TPU v7x, 32 devices: a whole 2x2x4 slice. The times are simulated.
32 devices in a mesh: gx: 8 (over z, y), gy: 4 (over x, core).
Axes of the slice: x: 2, y: 2, z: 4, core: 2. Of those that a mesh axis runs over, the one named last changes fastest.
Arguments:
- forces: float32 [3, 128, 128, 256], P(None, 'gx', 'gy'), may hold values from -8 to 8
- pressure_prev: float32 [128, 128, 256], P('gx', 'gy'), may hold values from -8 to 8
Outputs:
- pressure: float32 [128, 128, 256], P('gx', 'gy')
- residual: float32 [128, 128, 256], P('gx', 'gy')
All inputs are finite; a program needn't handle non-finite values.
Results may differ from a plain program's by a relative error of at most 0.0003.
Values sent between devices are 32-bit elements; how exact they have to be, the bound alone decides.
A program may use at most 64 MiB of HBM per device.

v0:
```python
import functools

import jax
import jax.numpy as jnp
from jax import lax
from jax.experimental import pallas as pl
from jax.experimental.pallas import tpu as pltpu
from jax.sharding import PartitionSpec as P

OMEGA = 0.8
PAD = 8
MESH = pl.DeviceIdType.MESH


def loop(count, body):
    def step(i, carry):
        body(i)
        return carry

    lax.fori_loop(0, count, step, 0)


def vertical(c):
    depth = c.shape[-1]
    axis = c.ndim - 1
    lane = lax.broadcasted_iota(jnp.int32, c.shape, axis)
    below = jnp.where(lane == 0, 0.0, pltpu.roll(c, 1, axis))
    above = jnp.where(lane == depth - 1, 0.0, pltpu.roll(c, depth - 1, axis))
    return below + above


def parts(ref, row, count):
    block = ref[pl.ds(row - 1, count + 2)]
    c = block[1:-1]
    width = c.shape[1]
    lateral = (block[:-2] + block[2:]) + (pltpu.roll(c, 1, 1) + pltpu.roll(c, width - 1, 1))
    return c, lateral, vertical(c)


def sweep(src, f, dst, row, rows, weight, unit, cols=None):
    k = OMEGA / (4.0 * weight + 2.0)

    def body(i):
        r = row + i * unit
        c, lateral, up = parts(src, r, unit)
        new = (1.0 - OMEGA) * c + k * (weight * lateral + up + f[pl.ds(r, unit)])
        if cols is None:
            dst[pl.ds(r, unit)] = new
        else:
            dst[pl.ds(r, unit), cols[0] : cols[1]] = new[:, cols[0] : cols[1]]

    loop(rows // unit, body)


def sweep_twice_from_zero(f, dst, row, rows, weight, unit):
    k = OMEGA / (4.0 * weight + 2.0)

    def body(i):
        r = row + i * unit
        c, lateral, up = parts(f, r, unit)
        dst[pl.ds(r, unit)] = k * ((2.0 - OMEGA) * c + k * (weight * lateral + up))

    loop(rows // unit, body)


def residual_rows(v, f, r, count, weight):
    c, lateral, up = parts(v, r, count)
    return f[pl.ds(r, count)] - ((4.0 * weight + 2.0) * c - weight * lateral - up)


def restricted(v, f, tmp, row, rows, cols, weight, put):
    start, count = cols
    depth = v.shape[-1]

    def body(i):
        r = residual_rows(v, f, row + 2 * i, 2, weight)
        both = r[0] + r[1]
        width = both.shape[0]
        halves = []
        for h in range(depth // 128):
            tmp[h, 0:width] = both[:, h * 128 : (h + 1) * 128]
            halves.append(
                tmp[h, pl.ds(start, count // 2, 2)] + tmp[h, pl.ds(start + 1, count // 2, 2)]
            )
        put(i, 0.25 * jnp.concatenate(halves, axis=1))

    loop(rows // 2, body)


def doubled(e, tmp, start):
    width, depth = e.shape
    for h in range(depth // 128):
        piece = e[:, h * 128 : (h + 1) * 128]
        tmp[h, pl.ds(start, width, 2)] = piece
        tmp[h, pl.ds(start + 1, width, 2)] = piece


def read_tmp(tmp, start, width):
    return jnp.concatenate([tmp[h, pl.ds(start, width)] for h in range(tmp.shape[0])], axis=1)


def ghosts(v, rows):
    v[0] = v[rows]
    v[rows + 1] = v[1]


def kernel(
    nx, ny, cycles,
    forces, pressure, out_p, out_r,
    fx, fy, fz, s, pa, pb, t0, t1, res,
    f1a, f1b, v1a, v1b, f2a, f2b, v2a, v2b, f3, v3a, v3b, f4, v4a, v4b, green, tmp,
    local_sem, plane_send, plane_recv, halo_send, halo_recv,
    g_send, g_recv, h_send, h_recv,
):
    mx, my = lax.axis_index("gx"), lax.axis_index("gy")
    n = nx * ny
    me = mx * ny + my
    bx, by, depth = pressure.shape
    cx1, cy1 = bx // 2, by // 2
    cx2, cy2 = bx // 4, by // 4

    loads = [
        pltpu.make_async_copy(forces.at[0], fx.at[pl.ds(1, bx)], local_sem.at[0]),
        pltpu.make_async_copy(forces.at[1], fy.at[:, pl.ds(PAD, by)], local_sem.at[1]),
        pltpu.make_async_copy(pressure, pa.at[pl.ds(PAD, bx), pl.ds(PAD, by)], local_sem.at[2]),
        pltpu.make_async_copy(forces.at[2], fz, local_sem.at[3]),
    ]
    for load in loads:
        load.start()

    barrier = pltpu.get_barrier_semaphore()

    def greet(j):
        other = lax.rem(me + 1 + j, n)
        pl.semaphore_signal(barrier, inc=1, device_id=(other // ny, lax.rem(other, ny)), device_id_type=MESH)

    loop(n - 1, greet)

    row_i = lax.broadcasted_iota(jnp.int32, (depth, depth), 0).astype(jnp.float32)
    col_i = lax.broadcasted_iota(jnp.int32, (depth, depth), 1).astype(jnp.float32)
    green[...] = (jnp.minimum(row_i, col_i) + 1.0) * (depth - jnp.maximum(row_i, col_i)) / (depth + 1.0)

    pl.semaphore_wait(barrier, n - 1)

    sends = []

    def halo(ref, size, width, slot):
        sx, sy = size
        k = min(width, PAD)

        def strip(d, rows, cols, step):
            dx, dy = step
            copy = pltpu.make_async_remote_copy(
                src_ref=ref.at[rows[0], cols[0]],
                dst_ref=ref.at[rows[1], cols[1]],
                send_sem=halo_send.at[slot, d],
                recv_sem=halo_recv.at[slot, d],
                device_id=(lax.rem(mx + dx + nx, nx), lax.rem(my + dy + ny, ny)),
                device_id_type=MESH,
            )
            copy.start()
            sends.append(copy)
            return copy

        def rows_for(dx, w):
            if dx == 1:
                return pl.ds(PAD + sx - w, w), pl.ds(PAD - w, w)
            return pl.ds(PAD, w), pl.ds(PAD + sx, w)

        rows = (pl.ds(PAD, sx), pl.ds(PAD, sx))
        cols = (pl.ds(PAD, sy), pl.ds(PAD, sy))
        low, high = pl.ds(PAD - k, k), pl.ds(PAD + sy, k)
        beside = [
            strip(0, rows, (pl.ds(PAD + sy - k, k), low), (0, 1)),
            strip(1, rows, (pl.ds(PAD, k), high), (0, -1)),
        ]
        late = [
            strip(2, rows_for(1, width), cols, (1, 0)),
            strip(3, rows_for(-1, width), cols, (-1, 0)),
        ]

        def corners():
            for copy in beside:
                copy.wait_recv()
            for d, (dx, side) in enumerate(((1, low), (1, high), (-1, low), (-1, high))):
                late.append(strip(4 + d, rows_for(dx, width - 1), (side, side), (dx, 0)))
            return late

        return corners

    def arrive(copies):
        for copy in copies:
            copy.wait_recv()

    right, above = lax.rem(mx + 1, nx), lax.rem(my + 1, ny)
    loads[0].wait()
    plane_x = pltpu.make_async_remote_copy(
        src_ref=fx.at[pl.ds(bx, 1)], dst_ref=fx.at[pl.ds(0, 1)],
        send_sem=plane_send.at[0], recv_sem=plane_recv.at[0],
        device_id=(right, my), device_id_type=MESH,
    )
    plane_x.start()
    loads[1].wait()
    plane_y = pltpu.make_async_remote_copy(
        src_ref=fy.at[:, pl.ds(PAD + by - 1, 1)], dst_ref=fy.at[:, pl.ds(PAD - 1, 1)],
        send_sem=plane_send.at[1], recv_sem=plane_recv.at[1],
        device_id=(mx, above), device_id_type=MESH,
    )
    plane_y.start()
    sends.extend([plane_x, plane_y])
    loads[2].wait()
    coming_p = halo(pa, (bx, by), 4, 0)
    loads[3].wait()
    plane_x.wait_recv()
    plane_y.wait_recv()

    def make_source(i):
        r = 2 * i
        x = fx[pl.ds(r, 3)]
        y = fy[pl.ds(r, 2)]
        z = fz[pl.ds(r, 2)]
        lane = lax.broadcasted_iota(jnp.int32, z.shape, 2)
        behind_z = jnp.where(lane == 0, 0.0, pltpu.roll(z, 1, 2))
        behind_y = pltpu.roll(y, 1, 1)[:, PAD:]
        s[pl.ds(PAD + r, 2), PAD : PAD + by] = (
            (x[:-1] - x[1:]) + (behind_y - y[:, PAD:]) + (behind_z - z)
        )

    loop(bx // 2, make_source)
    coming_s = halo(s, (bx, by), 4, 1)
    coming = coming_p() + coming_s()

    half = ny // 2
    many = nx * half
    parity = lax.rem(my, 2)
    partner = my + 1 - 2 * parity
    mine = mx * half + my // 2

    def solve_2(f2, turn):
        def place(x, y):
            return f2.at[pl.ds(1 + x * cx2, cx2), pl.ds(pl.multiple_of(y * cy2, cy2), cy2)]

        def direct(x, y, ident, to):
            return pltpu.make_async_remote_copy(
                src_ref=place(x, y), dst_ref=place(x, y),
                send_sem=g_send.at[turn, to], recv_sem=g_recv.at[turn, ident],
                device_id=(to // half, 2 * lax.rem(to, half) + parity), device_id_type=MESH,
            )

        def onward(x, y, ident):
            return pltpu.make_async_remote_copy(
                src_ref=place(x, y), dst_ref=place(x, y),
                send_sem=h_send.at[turn, ident], recv_sem=h_recv.at[turn, ident],
                device_id=(mx, partner), device_id_type=MESH,
            )

        def spot(ident, par):
            return ident // half, 2 * lax.rem(ident, half) + par

        def start(j):
            direct(mx, my, mine, lax.rem(mine + 1 + j, many)).start()

        loop(many - 1, start)
        onward(mx, my, mine).start()

        def pass_on(j):
            ident = lax.rem(mine + many - 1 - j, many)
            x, y = spot(ident, parity)
            direct(x, y, ident, ident).wait_recv()
            onward(x, y, ident).start()

        loop(many - 1, pass_on)

        def other(ident):
            x, y = spot(ident, 1 - parity)
            onward(x, y, ident).wait_recv()

        loop(many, other)

        def finish():
            def done(j):
                ident = lax.rem(mine + 1 + j, many)
                direct(mx, my, mine, ident).wait_send()
                x, y = spot(ident, parity)
                onward(x, y, ident).wait_send()

            loop(many - 1, done)
            onward(mx, my, mine).wait_send()

        sizes = [(cx2 * nx, cy2 * ny)]
        for _ in range(2):
            sizes.append((sizes[-1][0] // 2, sizes[-1][1] // 2))
        (x2, y2), (x3, y3), (x4, y4) = sizes

        ghosts(f2, x2)
        sweep_twice_from_zero(f2, v2a, 1, x2, 0.25**2, 4)
        ghosts(v2a, x2)

        def put3(i, value):
            f3[1 + i] = value

        restricted(v2a, f2, tmp, 1, x2, (0, y2), 0.25**2, put3)
        ghosts(f3, x3)
        sweep_twice_from_zero(f3, v3a, 1, x3, 0.25**3, 8)
        ghosts(v3a, x3)

        def put4(i, value):
            f4[1 + i] = value

        restricted(v3a, f3, tmp, 1, x3, (0, y3), 0.25**3, put4)
        total = jnp.sum(jnp.sum(f4[pl.ds(1, x4)], axis=0), axis=0, keepdims=True) / (x4 * y4)
        u = jnp.dot(
            jnp.broadcast_to(total, (8, depth)), green[...],
            preferred_element_type=jnp.float32, precision=lax.Precision.HIGHEST,
        )
        v4a[...] = jnp.broadcast_to(u[0:1][None], v4a.shape)
        for src, dst in ((v4a, v4b), (v4b, v4a), (v4a, v4b), (v4b, v4a)):
            sweep(src, f4, dst, 1, x4, 0.25**4, 8)
            ghosts(dst, x4)

        def climb(e, v, rows, width):
            def body(i):
                doubled(e[1 + i], tmp, 0)
                v[pl.ds(1 + 2 * i, 2)] += read_tmp(tmp, 0, 2 * width)[None]

            loop(rows, body)
            ghosts(v, 2 * rows)

        climb(v4a, v3a, x4, y4)
        sweep(v3a, f3, v3b, 1, x3, 0.25**3, 8)
        ghosts(v3b, x3)
        sweep(v3b, f3, v3a, 1, x3, 0.25**3, 8)
        climb(v3a, v2a, x3, y3)
        sweep(v2a, f2, v2b, 1, x2, 0.25**2, 4)
        ghosts(v2b, x2)
        sweep(v2b, f2, v2a, 1, x2, 0.25**2, 4)
        return finish

    ends = []
    for turn in range(cycles):
        last = turn == cycles - 1
        w = 5 if last else 4
        p_in, f1, f2 = (pa, f1a, f2a) if turn % 2 == 0 else (pb, f1b, f2b)
        inner = 1 + w % 2
        sweep(p_in, s, t0, PAD + inner, bx - 2 * inner, 1.0, 2)
        sweep(t0, s, t1, PAD + inner + 1, bx - 2 * inner - 2, 1.0, 2)
        arrive(coming)
        for src, dst, reach, off in ((p_in, t0, w - 1, inner), (t0, t1, w - 2, inner + 1)):
            sweep(src, s, dst, PAD - reach, reach + off, 1.0, 2)
            sweep(src, s, dst, PAD + bx - off, reach + off, 1.0, 2)

        def put1(i, value):
            f1[PAD + i, PAD : PAD + cy1] = value

        restricted(t1, s, tmp, PAD, bx, (PAD, by), 1.0, put1)
        coming = halo(f1, (cx1, cy1), 5, 2 + 2 * turn)()
        sweep_twice_from_zero(f1, v1a, PAD + 2, cx1 - 4, 0.25, 2)
        arrive(coming)
        sweep_twice_from_zero(f1, v1a, PAD - 4, 6, 0.25, 2)
        sweep_twice_from_zero(f1, v1a, PAD + cx1 - 2, 6, 0.25, 2)

        def put2(i, value):
            f2[1 + mx * cx2 + i, pl.ds(pl.multiple_of(my * cy2, cy2), cy2)] = value

        restricted(v1a, f1, tmp, PAD, cx1, (PAD, cy1), 0.25, put2)
        ends.append(solve_2(f2, turn))

        x2, y2 = cx2 * nx, cy2 * ny

        def down_to_1(i):
            q = lax.rem(mx * cx2 + i - 2 + x2, x2)
            doubled(v2a[1 + q], tmp, PAD)
            for h in range(tmp.shape[0]):
                tmp[h, 0:PAD] = tmp[h, 2 * y2 : 2 * y2 + PAD]
                tmp[h, 2 * y2 + PAD : 2 * y2 + 2 * PAD] = tmp[h, PAD : 2 * PAD]
            e = read_tmp(tmp, pl.multiple_of(my * cy1, PAD), cy1 + 2 * PAD)
            v1a[pl.ds(PAD - 4 + 2 * i, 2)] += e[None]

        loop(cx2 + 4, down_to_1)
        sweep(v1a, f1, v1b, PAD - 3, cx1 + 6, 0.25, 2)
        sweep(v1b, f1, v1a, PAD - 2, cx1 + 4, 0.25, 2)

        reach = 2 if last else 1

        def down_to_0(i):
            doubled(v1a[PAD - reach + i], tmp, 0)
            t1[pl.ds(PAD - 2 * reach + 2 * i, 2)] += read_tmp(tmp, PAD, by + 2 * PAD)[None]

        loop(cx1 + 2 * reach, down_to_0)
        sweep(t1, s, t0, PAD - (w - 3), bx + 2 * (w - 3), 1.0, 2)
        if last:
            sweep(t0, s, t1, PAD - 1, bx + 2, 1.0, 2)
        else:
            following = pb if turn % 2 == 0 else pa
            sweep(t0, s, following, PAD, bx, 1.0, 2, (PAD, PAD + by))
            coming = halo(following, (bx, by), 5, 3 + 2 * turn)()

    store_p = pltpu.make_async_copy(t1.at[pl.ds(PAD, bx), pl.ds(PAD, by)], out_p, local_sem.at[0])
    store_p.start()

    def last_residual(i):
        r = residual_rows(t1, s, PAD + 2 * i, 2, 1.0)
        res[pl.ds(2 * i, 2)] = r[:, PAD : PAD + by]

    loop(bx // 2, last_residual)
    store_r = pltpu.make_async_copy(res, out_r, local_sem.at[1])
    store_r.start()
    for copy in sends:
        copy.wait_send()
    for end in ends:
        end()
    store_p.wait()
    store_r.wait()


def on_device(nx, ny, forces, pressure_prev):
    bx, by, depth = pressure_prev.shape
    cycles = 2
    n = nx * ny
    f32 = jnp.float32

    def vmem(*shape):
        return pltpu.VMEM(shape + (depth,), f32)

    p0 = (bx + 2 * PAD, by + 2 * PAD)
    p1 = (bx // 2 + 2 * PAD, by // 2 + 2 * PAD)
    p2, p3, p4 = ((nx * bx // k + 2, ny * by // k) for k in (4, 8, 16))
    many = n // 2
    sem = pltpu.SemaphoreType.DMA
    scratch = (
        [vmem(bx + 1, by), vmem(bx, by + PAD), vmem(bx, by)]
        + [vmem(*p0)] * 5
        + [vmem(bx, by)]
        + [vmem(*p1)] * 4
        + [vmem(*p2)] * 4
        + [vmem(*p3)] * 3
        + [vmem(*p4)] * 3
        + [vmem(depth)]
        + [pltpu.VMEM((depth // 128, max(2 * p2[1], 2 * p1[1]) + 2 * PAD, 128), f32)]
        + [sem((4,)), sem((2,)), sem((2,))]
        + [sem((2 + 2 * cycles, 8))] * 2
        + [sem((cycles, many))] * 4
    )
    shape = jax.ShapeDtypeStruct((bx, by, depth), f32)
    anyspace = pl.BlockSpec(memory_space=pl.ANY)
    return pl.pallas_call(
        functools.partial(kernel, nx, ny, cycles),
        out_shape=(shape, shape),
        in_specs=[anyspace] * 2,
        out_specs=(anyspace, anyspace),
        scratch_shapes=scratch,
        compiler_params=pltpu.CompilerParams(
            collective_id=0, has_side_effects=True, vmem_limit_bytes=48 * 1024 * 1024
        ),
    )(forces, pressure_prev)


def solution(mesh):
    return jax.shard_map(
        functools.partial(on_device, mesh.shape["gx"], mesh.shape["gy"]),
        mesh=mesh,
        in_specs=(P(None, "gx", "gy", None), P("gx", "gy", None)),
        out_specs=(P("gx", "gy", None), P("gx", "gy", None)),
        check_vma=False,
    )
```

profile of v0, /device:TPU:0, one launch (start us, length us, event | category | flops | bytes accessed | tf_op | source)
XLA Modules:
  0.0 111.1 jit_solution(7913451618883445042)
XLA Ops:
  0.6 0.0 copy-start
  0.6 1.4 %copy-done = f32[3,16,32,256]{3,2,1,0:T(8,128)S(1)} copy-done((f32[3,16,32,256]{3,2,1,0:T(8,128)S(1)}, f32[3,16,32,256]{3,2,1,0:T(8,128)}, u32[]{:S(2)}) %copy-start) | copy-done | bytes 1572888
  2.0 0.0 copy-start.1
  2.0 1.0 copy-done.1
  3.1 106.5 %shard_map.41 = (f32[16,32,256]{2,1,0:T(8,128)S(1)}, f32[16,32,256]{2,1,0:T(8,128)S(1)}) custom-call(f32[3,16,32,256]{3,2,1,0:T(8,128)S(1)} %copy-done, f32[16,32,256]{2,1,0:T(8,128)S(1)} %copy-done.1), custom_call_target="tpu_custom_call" | custom-call | tf_op jit(solution)/shard_map/pallas_call | solution.py:446
  109.6 0.8 copy.6
  110.4 0.8 copy.7
Async XLA Ops:
  0.6 1.4 %copy-start = (f32[3,16,32,256]{3,2,1,0:T(8,128)S(1)}, f32[3,16,32,256]{3,2,1,0:T(8,128)}, u32[]{:S(2)}) copy-start(f32[3,16,32,256]{3,2,1,0:T(8,128)} %forces.1) | copy-start | bytes 4718596
  2.0 1.0 copy-start.1
where the time goes:
time: 113 us; the launch traced here: 111 us
  Pallas kernels  106 us (94%)
  local copies, waits for them, and re-layouts  4.03 us (4%)
    pallas_call x1, Pallas kernels, on_device(): pl.pallas_call(functools.partial(kernel, nx, ny, cycles), out_shape=(shap...  106 us
    unnamed x6, local copies, waits for them, and re-layouts  4.03 us

commit v1 on v0

v1 whole, which is shorter than its diff:
```python
import functools

import numpy as np

import jax
import jax.numpy as jnp
from jax import lax
from jax.experimental import pallas as pl
from jax.experimental.pallas import tpu as pltpu
from jax.sharding import PartitionSpec as P

OMEGA = 0.8
LEVELS = 5
CYCLES = 2
COARSE_SWEEPS = 4
PAD = 8
SUB = 8
LANES = 128
MESH = pl.DeviceIdType.MESH
EXACT = lax.Precision.HIGHEST


def loop(count, body):
    def step(i, carry):
        body(i)
        return carry

    lax.fori_loop(0, count, step, 0)


def lateral_rows(v, r, count, by):
    block = v[pl.ds(r, count + 2)]
    c = block[1:-1]
    width = c.shape[1]
    sides = pltpu.roll(c, 1, 1) + pltpu.roll(c, width - 1, 1)
    around = (block[:-2] + block[2:] + sides)[:, PAD : PAD + by]
    return 4.0 * c[:, PAD : PAD + by] - around


class Level:
    def __init__(self, index, rows, rate):
        self.rows, self.rate, self.shift = rows, rate, 2**index
        self.weight = 0.25**index
        self.k = OMEGA / (4.0 * self.weight + 2.0)
        self.unit = min(rows, 8)

    def sides(self, c):
        axis = c.ndim - 1
        return pltpu.roll(c, self.shift, axis) + pltpu.roll(c, c.shape[axis] - self.shift, axis)

    def relax(self, c, lateral, f):
        keep = 1.0 - self.k * (4.0 * self.weight + self.rate)
        return keep * c + (self.k * self.weight) * lateral + self.k * f

    def begin(self, f, lateral):
        keep = self.k * (2.0 - self.k * (4.0 * self.weight + self.rate))
        return keep * f + (self.k * self.k * self.weight) * lateral

    def remainder(self, c, lateral, f):
        return (f - self.rate * c) - self.weight * (4.0 * c - lateral)

    def restrict(self, r):
        pairs = r.reshape((r.shape[0] // 2, 2) + r.shape[1:])
        s = pairs[:, 0] + pairs[:, 1]
        width = s.shape[2]
        lane = lax.broadcasted_iota(jnp.int32, s.shape, 2)
        odd = (lane & self.shift) != 0
        other = jnp.where(odd, pltpu.roll(s, self.shift, 2), pltpu.roll(s, width - self.shift, 2))
        return 0.25 * (s + other)

    def each(self, body):
        loop(self.rows // self.unit, lambda i: body(pl.multiple_of(i * self.unit, self.unit)))

    def around(self, ref, x):
        block = ref[pl.ds(x, self.unit + 2)]
        c = block[1:-1]
        return c, (block[:-2] + block[2:]) + self.sides(c)

    def ghosts(self, ref):
        ref[0] = ref[self.rows]
        ref[self.rows + 1] = ref[1]

    def sweep(self, v, f, dst):
        def body(x):
            c, lateral = self.around(v, x)
            dst[pl.ds(1 + x, self.unit)] = self.relax(c, lateral, f[pl.ds(1 + x, self.unit)])

        self.each(body)
        self.ghosts(dst)

    def sweep_twice_from_zero(self, f, dst):
        def body(x):
            c, lateral = self.around(f, x)
            dst[pl.ds(1 + x, self.unit)] = self.begin(c, lateral)

        self.each(body)
        self.ghosts(dst)

    def restricted(self, v, f, dst):
        def body(x):
            c, lateral = self.around(v, x)
            r = self.remainder(c, lateral, f[pl.ds(1 + x, self.unit)])
            dst[pl.ds(1 + x // 2, self.unit // 2)] = self.restrict(r)

        self.each(body)
        dst[0] = dst[self.rows // 2]
        dst[self.rows // 2 + 1] = dst[1]

    def corrected_sweep(self, v, e, f, dst):
        def body(x):
            block = v[pl.ds(x, self.unit + 2)]
            half = e[pl.ds(x // 2, self.unit // 2 + 2)]
            pieces = [half[i] for i in range(self.unit // 2 + 2)]
            twice = [pieces[0]] + [p for p in pieces[1:-1] for _ in range(2)] + [pieces[-1]]
            block = block + jnp.stack(twice)
            c = block[1:-1]
            lateral = (block[:-2] + block[2:]) + self.sides(c)
            dst[pl.ds(1 + x, self.unit)] = self.relax(c, lateral, f[pl.ds(1 + x, self.unit)])

        self.each(body)
        self.ghosts(dst)

    def whole(self, c):
        up = jnp.concatenate([c[-1:], c[:-1]], axis=0)
        down = jnp.concatenate([c[1:], c[:1]], axis=0)
        return (up + down) + self.sides(c)


def kernel(
    nx, ny,
    forces, pressure, sine_in, rates_in, out_p, out_r,
    fx, fy, fz, pa, da, r0, sine, rates, sb, rb, sb2, rb2,
    f0, a0, b0, f1, a1, b1, f2, a2, b2, f3, a3, b3, f4, a4,
    local_sem, plane_send, plane_recv, halo_send, halo_recv,
    go_send, go_recv, back_send, back_recv,
):
    mx, my = lax.axis_index("gx"), lax.axis_index("gy")
    n = nx * ny
    me = mx * ny + my
    bx, by, depth = pressure.shape
    tx = LANES // by
    tiles = bx // tx

    loads = [
        pltpu.make_async_copy(forces.at[0], fx.at[pl.ds(1, bx)], local_sem.at[0]),
        pltpu.make_async_copy(forces.at[1], fy.at[:, pl.ds(PAD, by)], local_sem.at[1]),
        pltpu.make_async_copy(pressure, pa.at[pl.ds(1, bx), pl.ds(PAD, by)], local_sem.at[2]),
        pltpu.make_async_copy(forces.at[2], fz, local_sem.at[3]),
        pltpu.make_async_copy(sine_in, sine, local_sem.at[4]),
        pltpu.make_async_copy(rates_in, rates, local_sem.at[5]),
    ]
    for load in loads:
        load.start()

    def device(d):
        return d // ny, lax.rem(d, ny)

    barrier = pltpu.get_barrier_semaphore()

    def greet(j):
        pl.semaphore_signal(
            barrier, inc=1, device_id=device(lax.rem(me + 1 + j, n)), device_id_type=MESH
        )

    loop(n - 1, greet)
    pl.semaphore_wait(barrier, n - 1)

    right, left = lax.rem(mx + 1, nx), lax.rem(mx + nx - 1, nx)
    above, below = lax.rem(my + 1, ny), lax.rem(my + ny - 1, ny)

    def remote(src, dst, send, recv, to):
        copy = pltpu.make_async_remote_copy(
            src_ref=src, dst_ref=dst, send_sem=send, recv_sem=recv,
            device_id=to, device_id_type=MESH,
        )
        copy.start()
        return copy

    def halo(ref, turn):
        inner = pl.ds(PAD, by)
        rows = pl.ds(1, bx)

        def strip(d, src, dst, to):
            return remote(src, dst, halo_send.at[turn, d], halo_recv.at[turn, d], to)

        return [
            strip(0, ref.at[pl.ds(bx, 1), inner], ref.at[pl.ds(0, 1), inner], (right, my)),
            strip(1, ref.at[pl.ds(1, 1), inner], ref.at[pl.ds(bx + 1, 1), inner], (left, my)),
            strip(2, ref.at[rows, pl.ds(PAD + by - 1, 1)], ref.at[rows, pl.ds(PAD - 1, 1)], (mx, above)),
            strip(3, ref.at[rows, pl.ds(PAD, 1)], ref.at[rows, pl.ds(PAD + by, 1)], (mx, below)),
        ]

    for load in loads[:3]:
        load.wait()
    early = halo(pa, 0)
    early.append(
        remote(fx.at[pl.ds(bx, 1)], fx.at[pl.ds(0, 1)], plane_send.at[0], plane_recv.at[0], (right, my))
    )
    early.append(
        remote(
            fy.at[:, pl.ds(PAD + by - 1, 1)], fy.at[:, pl.ds(PAD - 1, 1)],
            plane_send.at[1], plane_recv.at[1], (mx, above),
        )
    )
    for load in loads[3:]:
        load.wait()
    for copy in early:
        copy.wait_recv()

    def make_remainder(i):
        r = 2 * i
        x = fx[pl.ds(r, 3)]
        y = fy[pl.ds(r, 2)]
        z = fz[pl.ds(r, 2)]
        lane = lax.broadcasted_iota(jnp.int32, z.shape, 2)
        behind_z = jnp.where(lane == 0, 0.0, pltpu.roll(z, 1, 2))
        behind_y = pltpu.roll(y, 1, 1)[:, PAD:]
        source = (x[:-1] - x[1:]) + (behind_y - y[:, PAD:]) + (behind_z - z)
        r0[pl.ds(r, 2)] = source - lateral_rows(pa, r, 2, by)

    loop(bx // 2, make_remainder)

    every = rates[...]

    def to_modes(cells):
        return lax.dot_general(
            sine[...], cells.reshape(2 * LANES, depth), (((1,), (1,)), ((), ())),
            preferred_element_type=jnp.float32, precision=EXACT,
        )

    def forward(i):
        r = 2 * tx * i
        modes = to_modes(r0[pl.ds(r, 2 * tx)])
        start = to_modes(pa[pl.ds(1 + r, 2 * tx), PAD : PAD + by])
        for h in range(2):
            half = slice(h * LANES, (h + 1) * LANES)
            sb[:, 2 * i + h] = (modes[:, half] - every * start[:, half]).reshape(n, SUB, LANES)

    loop(tiles // 2, forward)

    def exchange(src, dst, send, recv):
        def message(d, slot):
            return pltpu.make_async_remote_copy(
                src_ref=src.at[d], dst_ref=dst.at[slot], send_sem=send.at[d], recv_sem=recv.at[slot],
                device_id=device(d), device_id_type=MESH,
            )

        def start(j):
            d = lax.rem(me + 1 + j, n)
            message(d, me).start()

        loop(n - 1, start)
        dst[me] = src[me]

        def arrive(j):
            d = lax.rem(me + 1 + j, n)
            message(d, d).wait_recv()

        loop(n - 1, arrive)

        def finish():
            def done(j):
                d = lax.rem(me + 1 + j, n)
                message(d, d).wait_send()

            loop(n - 1, done)

        return finish

    ends = [exchange(sb, rb, go_send, go_recv)]

    def assemble(q):
        gx, t = q // tiles, lax.rem(q, tiles)
        parts = [rb[gx * ny + g, t] for g in range(ny)]
        for i in range(tx):
            row = [part[:, i * by : (i + 1) * by] for part in parts]
            f0[1 + q * tx + i] = jnp.concatenate(row, axis=1)

    loop(nx * tiles, assemble)

    mine = rates[pl.ds(pl.multiple_of(me * SUB, SUB), SUB)]
    lam = jnp.concatenate([mine] * (ny * by // LANES), axis=1)
    rows = nx * bx
    l0, l1, l2, l3, l4 = (Level(i, rows // 2**i, lam) for i in range(LEVELS))
    l0.ghosts(f0)

    for cycle in range(CYCLES):
        if cycle == 0:
            l0.sweep_twice_from_zero(f0, a0)
        else:
            l0.sweep(a0, f0, b0)
            l0.sweep(b0, f0, a0)
        l0.restricted(a0, f0, f1)
        l1.sweep_twice_from_zero(f1, a1)
        l1.restricted(a1, f1, f2)
        l2.sweep_twice_from_zero(f2, a2)
        l2.restricted(a2, f2, f3)
        l3.sweep_twice_from_zero(f3, a3)
        l3.restricted(a3, f3, f4)
        f = f4[pl.ds(1, l4.rows)]
        mean = jnp.sum(jnp.sum(f, axis=0), axis=1, keepdims=True) / (l4.rows * f.shape[2])
        v = jnp.broadcast_to((mean / lam)[None], f.shape)
        for _ in range(COARSE_SWEEPS):
            v = l4.relax(v, l4.whole(v), f)
        a4[pl.ds(1, l4.rows)] = v
        l4.ghosts(a4)
        l3.corrected_sweep(a3, a4, f3, b3)
        l3.sweep(b3, f3, a3)
        l2.corrected_sweep(a2, a3, f2, b2)
        l2.sweep(b2, f2, a2)
        l1.corrected_sweep(a1, a2, f1, b1)
        l1.sweep(b1, f1, a1)
        l0.corrected_sweep(a0, a1, f0, b0)
        l0.sweep(b0, f0, a0)

    def disassemble(q):
        gx, t = q // tiles, lax.rem(q, tiles)
        block = a0[pl.ds(1 + q * tx, tx)]
        for g in range(ny):
            pieces = [block[i][:, g * by : (g + 1) * by] for i in range(tx)]
            sb2[gx * ny + g, t] = jnp.concatenate(pieces, axis=1)

    loop(nx * tiles, disassemble)
    ends.append(exchange(sb2, rb2, back_send, back_recv))

    def backward(mail, i):
        halves = [mail[:, 2 * i + h].reshape(n * SUB, LANES) for h in range(2)]
        cells = lax.dot_general(
            jnp.concatenate(halves, axis=1), sine[...], (((0,), (0,)), ((), ())),
            preferred_element_type=jnp.float32, precision=EXACT,
        )
        return cells.reshape(2 * tx, by, depth)

    def correction(i):
        d = backward(rb2, i)
        da[pl.ds(1 + 2 * tx * i, 2 * tx), PAD : PAD + by] = d
        r = 2 * tx * i
        out_p[pl.ds(r, 2 * tx)] = pa[pl.ds(1 + r, 2 * tx), PAD : PAD + by] + d

    loop(tiles // 2, correction)
    late = halo(da, 1)

    def inner_remainder(d):
        c = rb2[d]
        lane = lax.broadcasted_iota(jnp.int32, c.shape, 2)
        column = lax.rem(lane, by)
        zero = jnp.zeros_like(c[:1])
        after = pltpu.roll(c, LANES - by, 2)
        after = jnp.where(lane < LANES - by, after, jnp.concatenate([after[1:], zero], axis=0))
        before = pltpu.roll(c, by, 2)
        before = jnp.where(lane < by, jnp.concatenate([zero, before[:-1]], axis=0), before)
        after_y = jnp.where(column == by - 1, 0.0, pltpu.roll(c, LANES - 1, 2))
        before_y = jnp.where(column == 0, 0.0, pltpu.roll(c, 1, 2))
        lam = rates[pl.ds(pl.multiple_of(d * SUB, SUB), SUB)]
        rb[d] = (sb[d] - lam[None] * c) - (4.0 * c - ((after + before) + (after_y + before_y)))

    loop(n, inner_remainder)

    def remainder(i):
        out_r[pl.ds(2 * tx * i, 2 * tx)] = backward(rb, i)

    loop(tiles // 2, remainder)

    for copy in late:
        copy.wait_recv()

    inner = pl.ds(PAD, by)
    out_r[0] += da[0, inner]
    out_r[bx - 1] += da[bx + 1, inner]

    def edges(i):
        sub = lax.broadcasted_iota(jnp.int32, (1, PAD, depth), 1)
        r = pl.ds(i, 1)
        first = pltpu.roll(da[pl.ds(1 + i, 1), 0:PAD], 1, 1)
        out_r[r, 0:PAD] += jnp.where(sub == 0, first, 0.0)
        last = pltpu.roll(da[pl.ds(1 + i, 1), PAD + by : 2 * PAD + by], PAD - 1, 1)
        out_r[r, by - PAD : by] += jnp.where(sub == PAD - 1, last, 0.0)

    loop(bx, edges)
    for copy in early + late:
        copy.wait_send()
    for end in ends:
        end()


def transform(depth, n):
    per = -(-depth // n)
    index = np.arange(1, depth + 1)
    angle = np.pi / (depth + 1)
    sines = np.sqrt(2.0 / (depth + 1)) * np.sin(angle * (np.outer(index, index) % (2 * (depth + 1))))
    rates = 4.0 * np.sin(0.5 * angle * index) ** 2
    matrix = np.zeros((n, SUB, depth))
    column = np.ones((n, SUB))
    for m in range(depth):
        matrix[m // per, m % per] = sines[m]
        column[m // per, m % per] = rates[m]
    rows = np.repeat(column.reshape(n * SUB, 1), LANES, axis=1)
    return matrix.reshape(n * SUB, depth).astype(np.float32), rows.astype(np.float32)


def on_device(nx, ny, forces, pressure_prev):
    bx, by, depth = pressure_prev.shape
    n = nx * ny
    f32 = jnp.float32
    width = ny * by
    tx = LANES // by
    tiles = bx // tx
    sine, rates = transform(depth, n)

    def vmem(*shape):
        return pltpu.VMEM(shape, f32)

    sem = pltpu.SemaphoreType.DMA
    padded = (bx + 2, by + 2 * PAD, depth)
    mail = (n, tiles, SUB, LANES)
    levels = []
    for level in range(LEVELS):
        count = 3 if level < LEVELS - 1 else 2
        levels += [vmem(nx * bx // 2**level + 2, SUB, width)] * count
    scratch = (
        [vmem(bx + 1, by, depth), vmem(bx, by + PAD, depth), vmem(bx, by, depth)]
        + [vmem(*padded)] * 2
        + [vmem(bx, by, depth), vmem(n * SUB, depth), vmem(n * SUB, LANES)]
        + [vmem(*mail)] * 4
        + levels
        + [sem((6,)), sem((2,)), sem((2,)), sem((2, 4)), sem((2, 4))]
        + [sem((n,))] * 4
    )
    shape = jax.ShapeDtypeStruct((bx, by, depth), f32)
    anyspace = pl.BlockSpec(memory_space=pl.ANY)
    vmemspace = pl.BlockSpec(memory_space=pltpu.VMEM)
    return pl.pallas_call(
        functools.partial(kernel, nx, ny),
        out_shape=(shape, shape),
        in_specs=[anyspace] * 4,
        out_specs=(vmemspace, vmemspace),
        scratch_shapes=scratch,
        compiler_params=pltpu.CompilerParams(
            collective_id=0, has_side_effects=True, vmem_limit_bytes=60 * 1024 * 1024
        ),
    )(forces, pressure_prev, sine, rates)


def solution(mesh):
    return jax.shard_map(
        functools.partial(on_device, mesh.shape["gx"], mesh.shape["gy"]),
        mesh=mesh,
        in_specs=(P(None, "gx", "gy", None), P("gx", "gy", None)),
        out_specs=(P("gx", "gy", None), P("gx", "gy", None)),
        check_vma=False,
    )
```

time: 113 us -> 87.2 us (0.77); the launches traced: 111 us -> 87 us
  Pallas kernels: 106 us -> 82.6 us
    pallas_call x1, Pallas kernels: 106 us -> 82.6 us  [on_device(): pl.pallas_call(functools.partial(kernel, nx, ny), out_shape=(shape, shape...]
    unnamed x6 -> x2, local copies, waits for them, and re-layouts: 4.03 us -> 3.76 us
where the time goes in v1:
time: 87.2 us; the launch traced here: 87 us
  Pallas kernels  82.6 us (95%)
  local copies, waits for them, and re-layouts  3.76 us (4%)
    pallas_call x1, Pallas kernels, on_device(): pl.pallas_call(functools.partial(kernel, nx, ny), out_shape=(shape, shape...  82.6 us
    unnamed x2, local copies, waits for them, and re-layouts  3.76 us

profile of v1, /device:TPU:0, one launch (start us, length us, event | category | flops | bytes accessed | tf_op | source)
XLA Modules:
  0.0 87.0 jit_solution(10373239422807834905)
XLA Ops:
  0.6 82.6 %shard_map.59 = (f32[16,32,256]{2,1,0:T(8,128)}, f32[16,32,256]{2,1,0:T(8,128)}) custom-call(f32[3,16,32,256]{3,2,1,0:T(8,128)} %forces.1, f32[16,32,256]{2,1,0:T(8,128)} %pressure.1, f32[256,256]{1,0:T(8,128)} %constant.4.clone.sine_in, f32[256,128]{1,0:T(8,128)} %constant.5.clone.rates_in), custom_call_target="tpu_custom_call" | custom-call | tf_op jit(solution)/shard_map/pallas_call | solution.py:432
  83.2 1.9 %copy.8 = f32[16,32,256]{2,1,0:T(8,128)} copy(f32[16,32,256]{2,1,0:T(8,128)} %get-tuple-element.4) | data formatting | bytes 1048576
  85.1 1.9 %copy.9 = f32[16,32,256]{2,1,0:T(8,128)} copy(f32[16,32,256]{2,1,0:T(8,128)} %get-tuple-element.5) | data formatting | bytes 1048576

commit v2 on v1

v2 whole, which is shorter than its diff:
```python
import functools

import numpy as np

import jax
import jax.numpy as jnp
from jax import lax
from jax.experimental import pallas as pl
from jax.experimental.pallas import tpu as pltpu
from jax.sharding import PartitionSpec as P

OMEGA = 0.8
LEVELS = 5
CYCLES = 2
COARSE_SWEEPS = 4
SUB = 8
HALF = 4
LANES = 128
MESH = pl.DeviceIdType.MESH
EXACT = lax.Precision.HIGHEST


def loop(count, body):
    def step(i, carry):
        body(i)
        return carry

    lax.fori_loop(0, count, step, 0)


def low(shape):
    return lax.broadcasted_iota(jnp.int32, shape, len(shape) - 2) < HALF


def flip(c):
    return pltpu.roll(c, HALF, c.ndim - 2)


def swap(a, b):
    mask = low(a.shape)
    return jnp.where(mask, a, flip(b)), jnp.where(mask, flip(a), b)


def transposed(tiles, by):
    tiles = list(tiles)
    lane = lax.broadcasted_iota(jnp.int32, tiles[0].shape, tiles[0].ndim - 1)
    axis = tiles[0].ndim - 1
    step = 1
    while step < len(tiles):
        odd = (lane & (step * by)) != 0
        for g in range(len(tiles)):
            if g & step == 0:
                a, b = tiles[g], tiles[g + step]
                tiles[g] = jnp.where(odd, pltpu.roll(b, step * by, axis), a)
                tiles[g + step] = jnp.where(odd, b, pltpu.roll(a, LANES - step * by, axis))
        step *= 2
    return tiles


class Level:
    def __init__(self, index, rows, rate):
        self.rows, self.rate, self.shift = rows, rate, 2**index
        self.weight = 0.25**index
        self.k = OMEGA / (4.0 * self.weight + 2.0)
        self.unit = min(rows, 64 * LANES // rate.shape[1])

    def sides(self, c):
        axis = c.ndim - 1
        return pltpu.roll(c, self.shift, axis) + pltpu.roll(c, c.shape[axis] - self.shift, axis)

    def relax(self, c, lateral, f):
        keep = 1.0 - self.k * (4.0 * self.weight + self.rate)
        return keep * c + (self.k * self.weight) * lateral + self.k * f

    def begin(self, f, lateral):
        keep = self.k * (2.0 - self.k * (4.0 * self.weight + self.rate))
        return keep * f + (self.k * self.k * self.weight) * lateral

    def remainder(self, c, lateral, f):
        return (f - self.rate * c) - self.weight * (4.0 * c - lateral)

    def restrict(self, r):
        pairs = r.reshape((r.shape[0] // 2, 2) + r.shape[1:])
        s = pairs[:, 0] + pairs[:, 1]
        width = s.shape[2]
        lane = lax.broadcasted_iota(jnp.int32, s.shape, 2)
        odd = (lane & self.shift) != 0
        other = jnp.where(odd, pltpu.roll(s, self.shift, 2), pltpu.roll(s, width - self.shift, 2))
        return 0.25 * (s + other)

    def each(self, body):
        if self.unit == self.rows:
            body(0)
        else:
            loop(self.rows // self.unit, lambda i: body(pl.multiple_of(i * self.unit, self.unit)))

    def around(self, ref, x):
        block = ref[pl.ds(x, self.unit + 2)]
        c = block[1:-1]
        return c, (block[:-2] + block[2:]) + self.sides(c)

    def sweep(self, v, f, dst):
        def body(x):
            c, lateral = self.around(v, x)
            dst[pl.ds(1 + x, self.unit)] = self.relax(c, lateral, f[pl.ds(1 + x, self.unit)])

        self.each(body)
        ghosts(dst, self.rows)

    def sweep_twice_from_zero(self, f, dst):
        def body(x):
            c, lateral = self.around(f, x)
            dst[pl.ds(1 + x, self.unit)] = self.begin(c, lateral)

        self.each(body)
        ghosts(dst, self.rows)

    def restricted(self, v, f, dst):
        def body(x):
            c, lateral = self.around(v, x)
            r = self.remainder(c, lateral, f[pl.ds(1 + x, self.unit)])
            dst[pl.ds(1 + x // 2, self.unit // 2)] = self.restrict(r)

        self.each(body)
        ghosts(dst, self.rows // 2)

    def corrected_sweep(self, v, e, f, dst):
        def body(x):
            block = v[pl.ds(x, self.unit + 2)]
            half = e[pl.ds(x // 2, self.unit // 2 + 2)]
            pieces = [half[i] for i in range(self.unit // 2 + 2)]
            twice = [pieces[0]] + [p for p in pieces[1:-1] for _ in range(2)] + [pieces[-1]]
            block = block + jnp.stack(twice)
            c = block[1:-1]
            lateral = (block[:-2] + block[2:]) + self.sides(c)
            dst[pl.ds(1 + x, self.unit)] = self.relax(c, lateral, f[pl.ds(1 + x, self.unit)])

        self.each(body)
        ghosts(dst, self.rows)

    def solve(self, f):
        mean = jnp.sum(jnp.sum(f, axis=0), axis=1, keepdims=True)
        mean = (mean + flip(mean)) / (2 * self.rows * f.shape[2])
        v = jnp.broadcast_to((mean / self.rate)[None], f.shape)
        for _ in range(COARSE_SWEEPS):
            up = jnp.concatenate([flip(v[-1:]), v[:-1]], axis=0)
            down = jnp.concatenate([v[1:], flip(v[:1])], axis=0)
            v = self.relax(v, (up + down) + self.sides(v), f)
        return v


def ghosts(ref, rows):
    ref[0] = flip(ref[rows])
    ref[rows + 1] = flip(ref[1])


def kernel(
    nx, ny,
    forces, pressure, sine_in, decay_in, rates_in, out_p, out_r,
    fx, fy, fz, pa, da, g, sine, decay, rates, pre, sb, rb, sb2, rb2, ex, ey,
    f0, a0, b0, f1, a1, b1, f2, a2, b2, f3, a3, b3, f4, a4,
    local_sem, plane_send, plane_recv, halo_send, halo_recv,
    go_send, go_recv, back_send, back_recv,
):
    mx, my = lax.axis_index("gx"), lax.axis_index("gy")
    n = nx * ny
    me = mx * ny + my
    bx, by, depth = pressure.shape
    tx = LANES // by
    deep = bx // (2 * tx)
    cells = bx // 2 * by

    loads = [
        pltpu.make_async_copy(forces.at[0], fx.at[pl.ds(1, bx)], local_sem.at[0]),
        pltpu.make_async_copy(forces.at[1], fy, local_sem.at[1]),
        pltpu.make_async_copy(pressure, pa.at[pl.ds(1, bx)], local_sem.at[2]),
        pltpu.make_async_copy(forces.at[2], fz, local_sem.at[3]),
        pltpu.make_async_copy(sine_in, sine, local_sem.at[4]),
        pltpu.make_async_copy(decay_in, decay, local_sem.at[5]),
        pltpu.make_async_copy(rates_in, rates, local_sem.at[6]),
    ]
    for load in loads:
        load.start()

    def device(d):
        return d // ny, lax.rem(d, ny)

    barrier = pltpu.get_barrier_semaphore()

    def greet(j):
        pl.semaphore_signal(
            barrier, inc=1, device_id=device(lax.rem(me + 1 + j, n)), device_id_type=MESH
        )

    loop(n - 1, greet)
    fx[0] = jnp.zeros((by, depth), jnp.float32)
    pa[0] = jnp.zeros((by, depth), jnp.float32)
    pa[bx + 1] = jnp.zeros((by, depth), jnp.float32)
    for load in loads:
        load.wait()

    def make_source(i):
        r = 2 * i
        x = fx[pl.ds(r, 3)]
        y = fy[pl.ds(r, 2)]
        z = fz[pl.ds(r, 2)]
        p = pa[pl.ds(r, 4)]
        c = p[1:-1]
        lane = lax.broadcasted_iota(jnp.int32, z.shape, 2)
        column = lax.broadcasted_iota(jnp.int32, z.shape, 1)
        behind_z = jnp.where(lane == 0, 0.0, pltpu.roll(z, 1, 2))
        behind_y = jnp.where(column == 0, 0.0, pltpu.roll(y, 1, 1))
        source = (x[:-1] - x[1:]) + (behind_y - y) + (behind_z - z)
        before = jnp.where(column == 0, 0.0, pltpu.roll(c, 1, 1))
        after = jnp.where(column == by - 1, 0.0, pltpu.roll(c, by - 1, 1))
        around = (p[:-2] + p[2:]) + (before + after)
        g[pl.ds(r, 2)] = source - (4.0 * c - around)

    loop(bx // 2, make_source)

    def to_modes(matrix, rows):
        return lax.dot_general(
            matrix, rows.reshape(cells, depth), (((1,), (1,)), ((), ())),
            preferred_element_type=jnp.float32, precision=EXACT,
        )

    def prepare(q):
        h, c = q // 2, lax.rem(q, 2)
        pre[h, c] = to_modes(decay[h], pa[pl.ds(1 + c * (bx // 2), bx // 2)])

    loop(4, prepare)
    pl.semaphore_wait(barrier, n - 1)

    right, left = lax.rem(mx + 1, nx), lax.rem(mx + nx - 1, nx)
    above, below = lax.rem(my + 1, ny), lax.rem(my + ny - 1, ny)

    def remote(src, dst, send, recv, to):
        copy = pltpu.make_async_remote_copy(
            src_ref=src, dst_ref=dst, send_sem=send, recv_sem=recv,
            device_id=to, device_id_type=MESH,
        )
        copy.start()
        return copy

    rows = pl.ds(1, bx)

    def halo(ref, turn):
        def strip(d, src, dst, to):
            return remote(src, dst, halo_send.at[turn, d], halo_recv.at[turn, d], to)

        return [
            strip(0, ref.at[pl.ds(bx, 1)], ex.at[turn, pl.ds(0, 1)], (right, my)),
            strip(1, ref.at[pl.ds(1, 1)], ex.at[turn, pl.ds(1, 1)], (left, my)),
            strip(2, ref.at[rows, pl.ds(by - 1, 1)], ey.at[turn, :, pl.ds(0, 1)], (mx, above)),
            strip(3, ref.at[rows, pl.ds(0, 1)], ey.at[turn, :, pl.ds(SUB - 1, 1)], (mx, below)),
        ]

    def add_edges(ref, turn):
        ref[0] += ex[turn, 0]
        ref[bx - 1] += ex[turn, 1]
        sub = lax.broadcasted_iota(jnp.int32, (bx, SUB, depth), 1)
        ref[:, 0:SUB] += jnp.where(sub == 0, ey[turn], 0.0)
        ref[:, by - SUB : by] += jnp.where(sub == SUB - 1, ey[turn], 0.0)

    early = halo(pa, 0)
    early.append(
        remote(fx.at[pl.ds(bx, 1)], ex.at[2, pl.ds(0, 1)], plane_send.at[0], plane_recv.at[0], (right, my))
    )
    early.append(
        remote(
            fy.at[:, pl.ds(by - 1, 1)], ey.at[2, :, pl.ds(0, 1)],
            plane_send.at[1], plane_recv.at[1], (mx, above),
        )
    )
    for copy in early:
        copy.wait_recv()
    add_edges(g, 0)
    g[0] += ex[2, 0]
    column = lax.broadcasted_iota(jnp.int32, (bx, SUB, depth), 1)
    g[:, 0:SUB] += jnp.where(column == 0, ey[2], 0.0)

    class Exchange:
        def __init__(self, h, src, dst, send, recv):
            self.h, self.src, self.dst, self.send, self.recv = h, src, dst, send, recv

        def message(self, d, slot):
            h = self.h
            return pltpu.make_async_remote_copy(
                src_ref=self.src.at[h, d], dst_ref=self.dst.at[h, slot],
                send_sem=self.send.at[h, d], recv_sem=self.recv.at[h, slot],
                device_id=device(d), device_id_type=MESH,
            )

        def start(self):
            loop(n - 1, lambda j: self.message(lax.rem(me + 1 + j, n), me).start())
            self.dst[self.h, me] = self.src[self.h, me]

        def arrive(self):
            def one(j):
                d = lax.rem(me + n - 1 - j, n)
                self.message(d, d).wait_recv()

            loop(n - 1, one)

        def finish(self):
            def one(j):
                d = lax.rem(me + 1 + j, n)
                self.message(d, d).wait_send()

            loop(n - 1, one)

    def go(h):
        return Exchange(h, sb, rb, go_send, go_recv)

    def back(h):
        return Exchange(h, sb2, rb2, back_send, back_recv)

    def forward(h):
        modes = [to_modes(sine[h], g[pl.ds(c * (bx // 2), bx // 2)]) + pre[h, c] for c in range(2)]
        for p in range(deep):
            part = slice(p * LANES, (p + 1) * LANES)
            both = swap(*[m[:, part].reshape(n // 2, SUB, LANES) for m in modes])
            for parity in range(2):
                for e in range(n // 2):
                    sb[h, 2 * e + parity, p] = both[parity][e]
        go(h).start()

    loop(2, forward)

    def solve(h):
        go(h).arrive()
        for x in range(nx // 2):
            for p in range(deep):
                pairs = [swap(rb[h, x * ny + y, p], rb[h, (x + nx // 2) * ny + y, p]) for y in range(ny)]
                for c in range(2):
                    tiles = [pair[c] for pair in pairs]
                    groups = [transposed(tiles[k : k + tx], by) for k in range(0, ny, tx)]
                    first = 1 + x * bx + c * (bx // 2) + p * tx
                    for i in range(tx):
                        f0[first + i] = jnp.concatenate([group[i] for group in groups], axis=1)
        mine = rates[h, pl.ds(pl.multiple_of(me * SUB, SUB), SUB)]
        lam = jnp.concatenate([mine] * (ny * by // LANES), axis=1)
        count = nx * bx // 2
        l0, l1, l2, l3, l4 = (Level(i, count // 2**i, lam) for i in range(LEVELS))
        ghosts(f0, count)
        for cycle in range(CYCLES):
            if cycle == 0:
                l0.sweep_twice_from_zero(f0, a0)
            else:
                l0.sweep(a0, f0, b0)
                l0.sweep(b0, f0, a0)
            l0.restricted(a0, f0, f1)
            l1.sweep_twice_from_zero(f1, a1)
            l1.restricted(a1, f1, f2)
            l2.sweep_twice_from_zero(f2, a2)
            l2.restricted(a2, f2, f3)
            l3.sweep_twice_from_zero(f3, a3)
            l3.restricted(a3, f3, f4)
            a4[pl.ds(1, l4.rows)] = l4.solve(f4[pl.ds(1, l4.rows)])
            ghosts(a4, l4.rows)
            l3.corrected_sweep(a3, a4, f3, b3)
            l3.sweep(b3, f3, a3)
            l2.corrected_sweep(a2, a3, f2, b2)
            l2.sweep(b2, f2, a2)
            l1.corrected_sweep(a1, a2, f1, b1)
            l1.sweep(b1, f1, a1)
            l0.corrected_sweep(a0, a1, f0, b0)
            l0.sweep(b0, f0, a0)
        for x in range(nx // 2):
            for p in range(deep):
                kept = []
                for c in range(2):
                    first = 1 + x * bx + c * (bx // 2) + p * tx
                    block = a0[pl.ds(first, tx)]
                    tiles = []
                    for k in range(ny // tx):
                        part = slice(k * LANES, (k + 1) * LANES)
                        tiles += transposed([block[i][:, part] for i in range(tx)], by)
                    kept.append(tiles)
                for y in range(ny):
                    one, other = swap(kept[0][y], kept[1][y])
                    sb2[h, x * ny + y, p] = one
                    sb2[h, (x + nx // 2) * ny + y, p] = other
        back(h).start()

    loop(2, solve)

    def to_cells(mail, h):
        parts = [[], []]
        for p in range(deep):
            tiles = [
                swap(mail[h, 2 * e, p], mail[h, 2 * e + 1, p]) for e in range(n // 2)
            ]
            for c in range(2):
                parts[c].append(jnp.concatenate([t[c] for t in tiles], axis=0))
        for c in range(2):
            values = lax.dot_general(
                jnp.concatenate(parts[c], axis=1), sine[h], (((0,), (0,)), ((), ())),
                preferred_element_type=jnp.float32, precision=EXACT,
            )
            yield c * (bx // 2), values.reshape(bx // 2, by, depth)

    def inner_remainder(h, d):
        c = rb2[h, d]
        lane = lax.broadcasted_iota(jnp.int32, c.shape, 2)
        lower = low((1, SUB, LANES))
        column = lax.rem(lane, by)
        after = pltpu.roll(c, LANES - by, 2)
        beyond = jnp.where(lower, flip(after[:1]), 0.0)
        after = jnp.where(lane < LANES - by, after, jnp.concatenate([after[1:], beyond], axis=0))
        before = pltpu.roll(c, by, 2)
        beyond = jnp.where(lower, 0.0, flip(before[-1:]))
        before = jnp.where(lane < by, jnp.concatenate([beyond, before[:-1]], axis=0), before)
        after_y = jnp.where(column == by - 1, 0.0, pltpu.roll(c, LANES - 1, 2))
        before_y = jnp.where(column == 0, 0.0, pltpu.roll(c, 1, 2))
        lam = rates[h, pl.ds(pl.multiple_of(d * SUB, SUB), SUB)][None]
        rb[h, d] = (sb[h, d] - lam * c) - (4.0 * c - ((after + before) + (after_y + before_y)))

    def remainders(h):
        def several(i):
            for j in range(8):
                inner_remainder(h, 8 * i + j)

        loop(n // 8, several)

    half = bx // 2
    back(0).arrive()
    for r, values in to_cells(rb2, 0):
        da[pl.ds(1 + r, half)] = values
    remainders(0)
    for r, values in to_cells(rb, 0):
        out_r[pl.ds(r, half)] = values
    back(1).arrive()
    for r, values in to_cells(rb2, 1):
        da[pl.ds(1 + r, half)] += values
    late = halo(da, 1)
    remainders(1)
    for r, values in to_cells(rb, 1):
        out_r[pl.ds(r, half)] += values
    out_p[...] = pa[pl.ds(1, bx)] + da[pl.ds(1, bx)]
    for copy in late:
        copy.wait_recv()
    add_edges(out_r, 1)
    for copy in early + late:
        copy.wait_send()
    for h in range(2):
        go(h).finish()
        back(h).finish()


def transform(depth, n):
    per = -(-depth // n)
    each = -(-per // 2)
    index = np.arange(1, depth + 1)
    angle = np.pi / (depth + 1)
    sines = np.sqrt(2.0 / (depth + 1)) * np.sin(angle * (np.outer(index, index) % (2 * (depth + 1))))
    rates = 4.0 * np.sin(0.5 * angle * index) ** 2
    matrix = np.zeros((2, n, HALF, depth))
    column = np.ones((2, n, 2, HALF))
    decay = np.zeros((2, n, HALF, depth))
    for m in range(depth):
        d, h, j = m // per, m % per // each, m % per % each
        matrix[h, d, j] = sines[m]
        decay[h, d, j] = -rates[m] * sines[m]
        column[h, d, :, j] = rates[m]
    column = np.repeat(column.reshape(2, n * SUB, 1), LANES, axis=2)
    arrays = matrix.reshape(2, n * HALF, depth), decay.reshape(2, n * HALF, depth), column
    return [a.astype(np.float32) for a in arrays]


def on_device(nx, ny, forces, pressure_prev):
    bx, by, depth = pressure_prev.shape
    n = nx * ny
    f32 = jnp.float32
    width = ny * by
    tx = LANES // by
    deep = bx // (2 * tx)
    constants = transform(depth, n)

    def vmem(*shape):
        return pltpu.VMEM(shape, f32)

    sem = pltpu.SemaphoreType.DMA
    block = (bx, by, depth)
    levels = []
    for level in range(LEVELS):
        count = 3 if level < LEVELS - 1 else 2
        levels += [vmem(nx * bx // 2 // 2**level + 2, SUB, width)] * count
    scratch = (
        [vmem(bx + 1, by, depth), vmem(*block), vmem(*block)]
        + [vmem(bx + 2, by, depth)] * 2
        + [vmem(*block)]
        + [vmem(*c.shape) for c in constants]
        + [vmem(2, 2, n * HALF, bx // 2 * by)]
        + [vmem(2, n, deep, SUB, LANES)] * 4
        + [vmem(3, 2, by, depth), vmem(3, bx, SUB, depth)]
        + levels
        + [sem((7,)), sem((2,)), sem((2,)), sem((2, 4)), sem((2, 4))]
        + [sem((2, n))] * 4
    )
    shape = jax.ShapeDtypeStruct(block, f32)
    anyspace = pl.BlockSpec(memory_space=pl.ANY)
    vmemspace = pl.BlockSpec(memory_space=pltpu.VMEM)
    return pl.pallas_call(
        functools.partial(kernel, nx, ny),
        out_shape=(shape, shape),
        in_specs=[anyspace] * 5,
        out_specs=(vmemspace, vmemspace),
        scratch_shapes=scratch,
        compiler_params=pltpu.CompilerParams(
            collective_id=0, has_side_effects=True, vmem_limit_bytes=60 * 1024 * 1024
        ),
    )(forces, pressure_prev, *constants)


def solution(mesh):
    return jax.shard_map(
        functools.partial(on_device, mesh.shape["gx"], mesh.shape["gy"]),
        mesh=mesh,
        in_specs=(P(None, "gx", "gy", None), P("gx", "gy", None)),
        out_specs=(P("gx", "gy", None), P("gx", "gy", None)),
        check_vma=False,
    )
```

time: 87.2 us -> 57.8 us (0.66)
  Pallas kernels: 82.6 us -> 53.2 us
    pallas_call x1, Pallas kernels: 82.6 us -> 53.2 us  [on_device(): pl.pallas_call(functools.partial(kernel, nx, ny), out_shape=(shape, shape...]
where the time goes in v2:
time: 57.8 us; the launch traced here: 57.6 us
  Pallas kernels  53.2 us (92%)
  local copies, waits for them, and re-layouts  3.76 us (7%)
  between operations  0.64 us (1%)
    pallas_call x1, Pallas kernels, on_device(): pl.pallas_call(functools.partial(kernel, nx, ny), out_shape=(shape, shape...  53.2 us
    unnamed x2, local copies, waits for them, and re-layouts  3.76 us

profile of v2, /device:TPU:0, one launch (start us, length us, event | category | flops | bytes accessed | tf_op | source)
XLA Modules:
  0.0 57.6 jit_solution(3076255226630177770)
XLA Ops:
  0.6 53.2 %shard_map.68 = (f32[16,32,256]{2,1,0:T(8,128)}, f32[16,32,256]{2,1,0:T(8,128)}) custom-call(f32[3,16,32,256]{3,2,1,0:T(8,128)} %forces.1, f32[16,32,256]{2,1,0:T(8,128)} %pressure.1, f32[2,128,256]{2,1,0:T(8,128)} %constant.6.clone.sine_in, f32[2,128,256]{2,1,0:T(8,128)} %constant.7.clone.decay_in, f32[2,256,128]{2,1,0:T(8,128)} %constant.8.clone.rates_in), custom_call_target="tpu_custom_call" | custom-call | tf_op jit(solution)/shard_map/pallas_call | solution.py:504
  53.8 1.9 %copy.9 = f32[16,32,256]{2,1,0:T(8,128)} copy(f32[16,32,256]{2,1,0:T(8,128)} %get-tuple-element.4) | data formatting | bytes 1048576
  55.7 1.9 %copy.10 = f32[16,32,256]{2,1,0:T(8,128)} copy(f32[16,32,256]{2,1,0:T(8,128)} %get-tuple-element.5) | data formatting | bytes 1048576

commit v3 on v2

--- a/solution.py
+++ b/solution.py
@@ -58,35 +58,31 @@
 
 
 class Level:
-    def __init__(self, index, rows, rate):
-        self.rows, self.rate, self.shift = rows, rate, 2**index
+    def __init__(self, index, rows, rate, waves):
+        self.rows, self.rate = rows, rate
+        self.width = rate.shape[1]
+        self.period = self.width // 2**index
         self.weight = 0.25**index
         self.k = OMEGA / (4.0 * self.weight + 2.0)
-        self.unit = min(rows, 64 * LANES // rate.shape[1])
-
-    def sides(self, c):
-        axis = c.ndim - 1
-        return pltpu.roll(c, self.shift, axis) + pltpu.roll(c, c.shape[axis] - self.shift, axis)
-
-    def relax(self, c, lateral, f):
-        keep = 1.0 - self.k * (4.0 * self.weight + self.rate)
-        return keep * c + (self.k * self.weight) * lateral + self.k * f
-
-    def begin(self, f, lateral):
-        keep = self.k * (2.0 - self.k * (4.0 * self.weight + self.rate))
-        return keep * f + (self.k * self.k * self.weight) * lateral
-
-    def remainder(self, c, lateral, f):
-        return (f - self.rate * c) - self.weight * (4.0 * c - lateral)
+        self.unit = min(rows, 64 * LANES // self.width)
+        self.side, self.pair = (waves[i, pl.ds(index * SUB, SUB)] for i in range(2))
+
+    def symbol(self):
+        return self.k * (self.weight * self.side + self.rate)
+
+    def relax(self, c, beside, f):
+        return (1.0 - self.symbol()) * c + (self.k * self.weight) * beside + self.k * f
+
+    def begin(self, f, beside):
+        return (self.k * (2.0 - self.symbol())) * f + (self.k * self.k * self.weight) * beside
+
+    def remainder(self, c, beside, f):
+        return (f - self.rate * c) - self.weight * (self.side * c - beside)
 
     def restrict(self, r):
         pairs = r.reshape((r.shape[0] // 2, 2) + r.shape[1:])
-        s = pairs[:, 0] + pairs[:, 1]
-        width = s.shape[2]
-        lane = lax.broadcasted_iota(jnp.int32, s.shape, 2)
-        odd = (lane & self.shift) != 0
-        other = jnp.where(odd, pltpu.roll(s, self.shift, 2), pltpu.roll(s, width - self.shift, 2))
-        return 0.25 * (s + other)
+        s = (0.5 * self.pair) * (pairs[:, 0] + pairs[:, 1])
+        return s + pltpu.roll(s, self.period // 2, 2)
 
     def each(self, body):
         if self.unit == self.rows:
@@ -96,29 +92,28 @@
 
     def around(self, ref, x):
         block = ref[pl.ds(x, self.unit + 2)]
-        c = block[1:-1]
-        return c, (block[:-2] + block[2:]) + self.sides(c)
+        return block[1:-1], block[:-2] + block[2:]
 
     def sweep(self, v, f, dst):
         def body(x):
-            c, lateral = self.around(v, x)
-            dst[pl.ds(1 + x, self.unit)] = self.relax(c, lateral, f[pl.ds(1 + x, self.unit)])
+            c, beside = self.around(v, x)
+            dst[pl.ds(1 + x, self.unit)] = self.relax(c, beside, f[pl.ds(1 + x, self.unit)])
 
         self.each(body)
         ghosts(dst, self.rows)
 
     def sweep_twice_from_zero(self, f, dst):
         def body(x):
-            c, lateral = self.around(f, x)
-            dst[pl.ds(1 + x, self.unit)] = self.begin(c, lateral)
+            c, beside = self.around(f, x)
+            dst[pl.ds(1 + x, self.unit)] = self.begin(c, beside)
 
         self.each(body)
         ghosts(dst, self.rows)
 
     def restricted(self, v, f, dst):
         def body(x):
-            c, lateral = self.around(v, x)
-            r = self.remainder(c, lateral, f[pl.ds(1 + x, self.unit)])
+            c, beside = self.around(v, x)
+            r = self.remainder(c, beside, f[pl.ds(1 + x, self.unit)])
             dst[pl.ds(1 + x // 2, self.unit // 2)] = self.restrict(r)
 
         self.each(body)
@@ -127,25 +122,26 @@
     def corrected_sweep(self, v, e, f, dst):
         def body(x):
             block = v[pl.ds(x, self.unit + 2)]
-            half = e[pl.ds(x // 2, self.unit // 2 + 2)]
+            half = self.pair * e[pl.ds(x // 2, self.unit // 2 + 2)]
             pieces = [half[i] for i in range(self.unit // 2 + 2)]
             twice = [pieces[0]] + [p for p in pieces[1:-1] for _ in range(2)] + [pieces[-1]]
             block = block + jnp.stack(twice)
-            c = block[1:-1]
-            lateral = (block[:-2] + block[2:]) + self.sides(c)
-            dst[pl.ds(1 + x, self.unit)] = self.relax(c, lateral, f[pl.ds(1 + x, self.unit)])
+            c, beside = block[1:-1], block[:-2] + block[2:]
+            dst[pl.ds(1 + x, self.unit)] = self.relax(c, beside, f[pl.ds(1 + x, self.unit)])
 
         self.each(body)
         ghosts(dst, self.rows)
 
     def solve(self, f):
-        mean = jnp.sum(jnp.sum(f, axis=0), axis=1, keepdims=True)
-        mean = (mean + flip(mean)) / (2 * self.rows * f.shape[2])
-        v = jnp.broadcast_to((mean / self.rate)[None], f.shape)
+        mean = jnp.sum(f, axis=0)
+        mean = (mean + flip(mean)) / (2 * self.rows)
+        lane = lax.broadcasted_iota(jnp.int32, mean.shape, 1)
+        mean = jnp.where(lax.rem(lane, self.period) == 0, mean / self.rate, 0.0)
+        v = jnp.broadcast_to(mean[None], f.shape)
         for _ in range(COARSE_SWEEPS):
             up = jnp.concatenate([flip(v[-1:]), v[:-1]], axis=0)
             down = jnp.concatenate([v[1:], flip(v[:1])], axis=0)
-            v = self.relax(v, (up + down) + self.sides(v), f)
+            v = self.relax(v, up + down, f)
         return v
 
 
@@ -156,8 +152,8 @@
 
 def kernel(
     nx, ny,
-    forces, pressure, sine_in, decay_in, rates_in, out_p, out_r,
-    fx, fy, fz, pa, da, g, sine, decay, rates, pre, sb, rb, sb2, rb2, ex, ey,
+    forces, pressure, tables, out_p, out_r,
+    fx, fy, fz, pa, da, g, sine, decay, rates, hartley, waves, pre, sb, rb, sb2, rb2, ex, ey,
     f0, a0, b0, f1, a1, b1, f2, a2, b2, f3, a3, b3, f4, a4,
     local_sem, plane_send, plane_recv, halo_send, halo_recv,
     go_send, go_recv, back_send, back_recv,
@@ -175,10 +171,14 @@
         pltpu.make_async_copy(forces.at[1], fy, local_sem.at[1]),
         pltpu.make_async_copy(pressure, pa.at[pl.ds(1, bx)], local_sem.at[2]),
         pltpu.make_async_copy(forces.at[2], fz, local_sem.at[3]),
-        pltpu.make_async_copy(sine_in, sine, local_sem.at[4]),
-        pltpu.make_async_copy(decay_in, decay, local_sem.at[5]),
-        pltpu.make_async_copy(rates_in, rates, local_sem.at[6]),
     ]
+    at = 0
+    for ref in (sine, decay, rates, hartley, waves):
+        for h in range(2):
+            count, width = ref.shape[1:]
+            part = tables.at[pl.ds(at, count), pl.ds(0, width)]
+            loads.append(pltpu.make_async_copy(part, ref.at[h], local_sem.at[len(loads)]))
+            at += count
     for load in loads:
         load.start()
 
@@ -196,7 +196,52 @@
     fx[0] = jnp.zeros((by, depth), jnp.float32)
     pa[0] = jnp.zeros((by, depth), jnp.float32)
     pa[bx + 1] = jnp.zeros((by, depth), jnp.float32)
-    for load in loads:
+    for load in loads[:3]:
+        load.wait()
+    pl.semaphore_wait(barrier, n - 1)
+
+    right, left = lax.rem(mx + 1, nx), lax.rem(mx + nx - 1, nx)
+    above, below = lax.rem(my + 1, ny), lax.rem(my + ny - 1, ny)
+
+    def remote(src, dst, send, recv, to):
+        copy = pltpu.make_async_remote_copy(
+            src_ref=src, dst_ref=dst, send_sem=send, recv_sem=recv,
+            device_id=to, device_id_type=MESH,
+        )
+        copy.start()
+        return copy
+
+    rows = pl.ds(1, bx)
+
+    def halo(ref, turn):
+        def strip(d, src, dst, to):
+            return remote(src, dst, halo_send.at[turn, d], halo_recv.at[turn, d], to)
+
+        return [
+            strip(0, ref.at[pl.ds(bx, 1)], ex.at[turn, pl.ds(0, 1)], (right, my)),
+            strip(1, ref.at[pl.ds(1, 1)], ex.at[turn, pl.ds(1, 1)], (left, my)),
+            strip(2, ref.at[rows, pl.ds(by - 1, 1)], ey.at[turn, :, pl.ds(0, 1)], (mx, above)),
+            strip(3, ref.at[rows, pl.ds(0, 1)], ey.at[turn, :, pl.ds(SUB - 1, 1)], (mx, below)),
+        ]
+
+    def add_edges(ref, turn):
+        ref[0] += ex[turn, 0]
+        ref[bx - 1] += ex[turn, 1]
+        sub = lax.broadcasted_iota(jnp.int32, (bx, SUB, depth), 1)
+        ref[:, 0:SUB] += jnp.where(sub == 0, ey[turn], 0.0)
+        ref[:, by - SUB : by] += jnp.where(sub == SUB - 1, ey[turn], 0.0)
+
+    early = halo(pa, 0)
+    early.append(
+        remote(fx.at[pl.ds(bx, 1)], ex.at[2, pl.ds(0, 1)], plane_send.at[0], plane_recv.at[0], (right, my))
+    )
+    early.append(
+        remote(
+            fy.at[:, pl.ds(by - 1, 1)], ey.at[2, :, pl.ds(0, 1)],
+            plane_send.at[1], plane_recv.at[1], (mx, above),
+        )
+    )
+    for load in loads[3:]:
         load.wait()
 
     def make_source(i):
@@ -229,49 +274,6 @@
         pre[h, c] = to_modes(decay[h], pa[pl.ds(1 + c * (bx // 2), bx // 2)])
 
     loop(4, prepare)
-    pl.semaphore_wait(barrier, n - 1)
-
-    right, left = lax.rem(mx + 1, nx), lax.rem(mx + nx - 1, nx)
-    above, below = lax.rem(my + 1, ny), lax.rem(my + ny - 1, ny)
-
-    def remote(src, dst, send, recv, to):
-        copy = pltpu.make_async_remote_copy(
-            src_ref=src, dst_ref=dst, send_sem=send, recv_sem=recv,
-            device_id=to, device_id_type=MESH,
-        )
-        copy.start()
-        return copy
-
-    rows = pl.ds(1, bx)
-
-    def halo(ref, turn):
-        def strip(d, src, dst, to):
-            return remote(src, dst, halo_send.at[turn, d], halo_recv.at[turn, d], to)
-
-        return [
-            strip(0, ref.at[pl.ds(bx, 1)], ex.at[turn, pl.ds(0, 1)], (right, my)),
-            strip(1, ref.at[pl.ds(1, 1)], ex.at[turn, pl.ds(1, 1)], (left, my)),
-            strip(2, ref.at[rows, pl.ds(by - 1, 1)], ey.at[turn, :, pl.ds(0, 1)], (mx, above)),
-            strip(3, ref.at[rows, pl.ds(0, 1)], ey.at[turn, :, pl.ds(SUB - 1, 1)], (mx, below)),
-        ]
-
-    def add_edges(ref, turn):
-        ref[0] += ex[turn, 0]
-        ref[bx - 1] += ex[turn, 1]
-        sub = lax.broadcasted_iota(jnp.int32, (bx, SUB, depth), 1)
-        ref[:, 0:SUB] += jnp.where(sub == 0, ey[turn], 0.0)
-        ref[:, by - SUB : by] += jnp.where(sub == SUB - 1, ey[turn], 0.0)
-
-    early = halo(pa, 0)
-    early.append(
-        remote(fx.at[pl.ds(bx, 1)], ex.at[2, pl.ds(0, 1)], plane_send.at[0], plane_recv.at[0], (right, my))
-    )
-    early.append(
-        remote(
-            fy.at[:, pl.ds(by - 1, 1)], ey.at[2, :, pl.ds(0, 1)],
-            plane_send.at[1], plane_recv.at[1], (mx, above),
-        )
-    )
     for copy in early:
         copy.wait_recv()
     add_edges(g, 0)
@@ -283,31 +285,36 @@
         def __init__(self, h, src, dst, send, recv):
             self.h, self.src, self.dst, self.send, self.recv = h, src, dst, send, recv
 
-        def message(self, d, slot):
-            h = self.h
+        def copy(self, src, dst, to):
             return pltpu.make_async_remote_copy(
-                src_ref=self.src.at[h, d], dst_ref=self.dst.at[h, slot],
-                send_sem=self.send.at[h, d], recv_sem=self.recv.at[h, slot],
-                device_id=device(d), device_id_type=MESH,
+                src_ref=src, dst_ref=dst, send_sem=self.send.at[self.h], recv_sem=self.recv.at[self.h],
+                device_id=to, device_id_type=MESH,
             )
 
         def start(self):
-            loop(n - 1, lambda j: self.message(lax.rem(me + 1 + j, n), me).start())
+            src, dst = self.src.at[self.h], self.dst.at[self.h]
+
+            def column(i, first):
+                x = mx + i
+                x = jnp.where(x >= nx, x - nx, x)
+                for j in range(first, ny):
+                    y = my + j
+                    y = jnp.where(y >= ny, y - ny, y)
+                    self.copy(src.at[x * ny + y], dst.at[me], (x, y)).start()
+
+            loop(nx - 1, lambda i: column(i + 1, 0))
+            column(0, 1)
             self.dst[self.h, me] = self.src[self.h, me]
 
+        def all(self):
+            most = pl.ds(0, n - 1)
+            return self.copy(self.src.at[self.h, most], self.dst.at[self.h, most], (left, my))
+
         def arrive(self):
-            def one(j):
-                d = lax.rem(me + n - 1 - j, n)
-                self.message(d, d).wait_recv()
-
-            loop(n - 1, one)
+            self.all().wait_recv()
 
         def finish(self):
-            def one(j):
-                d = lax.rem(me + 1 + j, n)
-                self.message(d, d).wait_send()
-
-            loop(n - 1, one)
+            self.all().wait_send()
 
     def go(h):
         return Exchange(h, sb, rb, go_send, go_recv)
@@ -341,7 +348,16 @@
         mine = rates[h, pl.ds(pl.multiple_of(me * SUB, SUB), SUB)]
         lam = jnp.concatenate([mine] * (ny * by // LANES), axis=1)
         count = nx * bx // 2
-        l0, l1, l2, l3, l4 = (Level(i, count // 2**i, lam) for i in range(LEVELS))
+        l0, l1, l2, l3, l4 = (Level(i, count // 2**i, lam, waves) for i in range(LEVELS))
+        inner = pl.ds(1, count)
+
+        def along_y(ref, direction):
+            return lax.dot_general(
+                ref[inner].reshape(count * SUB, ny * by), hartley[direction], (((1,), (0,)), ((), ())),
+                preferred_element_type=jnp.float32, precision=EXACT,
+            ).reshape(count, SUB, ny * by)
+
+        f0[inner] = along_y(f0, 0)
         ghosts(f0, count)
         for cycle in range(CYCLES):
             if cycle == 0:
@@ -366,12 +382,13 @@
             l1.sweep(b1, f1, a1)
             l0.corrected_sweep(a0, a1, f0, b0)
             l0.sweep(b0, f0, a0)
+        b0[inner] = along_y(a0, 1)
         for x in range(nx // 2):
             for p in range(deep):
                 kept = []
                 for c in range(2):
                     first = 1 + x * bx + c * (bx // 2) + p * tx
-                    block = a0[pl.ds(first, tx)]
+                    block = b0[pl.ds(first, tx)]
                     tiles = []
                     for k in range(ny // tx):
                         part = slice(k * LANES, (k + 1) * LANES)
@@ -448,7 +465,7 @@
         back(h).finish()
 
 
-def transform(depth, n):
+def transform(depth, n, width):
     per = -(-depth // n)
     each = -(-per // 2)
     index = np.arange(1, depth + 1)
@@ -464,8 +481,25 @@
         decay[h, d, j] = -rates[m] * sines[m]
         column[h, d, :, j] = rates[m]
     column = np.repeat(column.reshape(2, n * SUB, 1), LANES, axis=2)
-    arrays = matrix.reshape(2, n * HALF, depth), decay.reshape(2, n * HALF, depth), column
-    return [a.astype(np.float32) for a in arrays]
+    angle = 2 * np.pi / (2 * width) * (np.outer(np.arange(width), 2 * np.arange(width) + 1) % (2 * width))
+    cas = np.cos(angle) + np.sin(angle)
+    waves = np.zeros((2, LEVELS, SUB, width))
+    for level in range(LEVELS):
+        period = width // 2**level
+        q = np.arange(width) % period
+        waves[0, level] = 4.0 - 2.0 * np.cos(2 * np.pi * q / period)
+        waves[1, level] = np.cos(np.pi * q / period) * np.where(2 * q < period, 1.0, -1.0)
+    hartley = np.stack([cas.T / width, cas])
+    return [
+        matrix.reshape(2, n * HALF, depth), decay.reshape(2, n * HALF, depth), column,
+        hartley, waves.reshape(2, LEVELS * SUB, width),
+    ]
+
+
+def stacked(arrays):
+    wide = max(a.shape[2] for a in arrays)
+    padded = [np.pad(a, ((0, 0), (0, 0), (0, wide - a.shape[2]))) for a in arrays]
+    return np.concatenate([half for a in padded for half in a]).astype(np.float32)
 
 
 def on_device(nx, ny, forces, pressure_prev):
@@ -475,7 +509,7 @@
     width = ny * by
     tx = LANES // by
     deep = bx // (2 * tx)
-    constants = transform(depth, n)
+    constants = transform(depth, n, width)
 
     def vmem(*shape):
         return pltpu.VMEM(shape, f32)
@@ -495,22 +529,22 @@
         + [vmem(2, n, deep, SUB, LANES)] * 4
         + [vmem(3, 2, by, depth), vmem(3, bx, SUB, depth)]
         + levels
-        + [sem((7,)), sem((2,)), sem((2,)), sem((2, 4)), sem((2, 4))]
-        + [sem((2, n))] * 4
+        + [sem((14,)), sem((2,)), sem((2,)), sem((2, 4)), sem((2, 4))]
+        + [sem((2,))] * 4
     )
     shape = jax.ShapeDtypeStruct(block, f32)
-    anyspace = pl.BlockSpec(memory_space=pl.ANY)
+    hbmspace = pl.BlockSpec(memory_space=pltpu.HBM)
     vmemspace = pl.BlockSpec(memory_space=pltpu.VMEM)
     return pl.pallas_call(
         functools.partial(kernel, nx, ny),
         out_shape=(shape, shape),
-        in_specs=[anyspace] * 5,
+        in_specs=[hbmspace] * 3,
         out_specs=(vmemspace, vmemspace),
         scratch_shapes=scratch,
         compiler_params=pltpu.CompilerParams(
-            collective_id=0, has_side_effects=True, vmem_limit_bytes=60 * 1024 * 1024
+            collective_id=0, has_side_effects=True, vmem_limit_bytes=67043328 - int(11.2 * 1024 * 1024)
         ),
-    )(forces, pressure_prev, *constants)
+    )(forces, pressure_prev, stacked(constants))
 
 
 def solution(mesh):

time: 57.8 us -> 46.6 us (0.81)
  Pallas kernels: 53.2 us -> 44.2 us
  local copies, waits for them, and re-layouts: 3.76 us -> 1.59 us
    pallas_call x1, Pallas kernels: 53.2 us -> 44.2 us  [on_device(): pl.pallas_call(functools.partial(kernel, nx, ny), out_shape=(shape, shape...]
    unnamed x2, local copies, waits for them, and re-layouts: 3.76 us -> 1.59 us
where the time goes in v3:
time: 46.6 us; the launch traced here: 46.4 us
  Pallas kernels  44.2 us (95%)
  local copies, waits for them, and re-layouts  1.59 us (3%)
  between operations  0.64 us (1%)
    pallas_call x1, Pallas kernels, on_device(): pl.pallas_call(functools.partial(kernel, nx, ny), out_shape=(shape, shape...  44.2 us
    unnamed x2, local copies, waits for them, and re-layouts  1.59 us

profile of v3, /device:TPU:0, one launch (start us, length us, event | category | flops | bytes accessed | tf_op | source)
XLA Modules:
  0.0 46.4 jit_solution(12523840304969572967)
XLA Ops:
  0.6 44.2 %shard_map.50 = (f32[16,32,256]{2,1,0:T(8,128)S(1)}, f32[16,32,256]{2,1,0:T(8,128)S(1)}) custom-call(f32[3,16,32,256]{3,2,1,0:T(8,128)} %forces.1, f32[16,32,256]{2,1,0:T(8,128)} %pressure.1, f32[1360,256]{1,0:T(8,128)} %constant.2.clone.tables), custom_call_target="tpu_custom_call" | custom-call | tf_op jit(solution)/shard_map/pallas_call | solution.py:538
  44.8 0.8 %copy.7 = f32[16,32,256]{2,1,0:T(8,128)} copy(f32[16,32,256]{2,1,0:T(8,128)S(1)} %get-tuple-element.4) | data formatting | bytes 1048576
  45.6 0.8 %copy.8 = f32[16,32,256]{2,1,0:T(8,128)} copy(f32[16,32,256]{2,1,0:T(8,128)S(1)} %get-tuple-element.5) | data formatting | bytes 1048576

commit v4 on v3

--- a/solution.py
+++ b/solution.py
@@ -57,6 +57,10 @@
     return tiles
 
 
+def tile(mail, h, d, p):
+    return mail[h, d, pl.ds(p * SUB, SUB)]
+
+
 class Level:
     def __init__(self, index, rows, rate, waves):
         self.rows, self.rate = rows, rate
@@ -153,7 +157,7 @@
 def kernel(
     nx, ny,
     forces, pressure, tables, out_p, out_r,
-    fx, fy, fz, pa, da, g, sine, decay, rates, hartley, waves, pre, sb, rb, sb2, rb2, ex, ey,
+    fx, fy, fz, pa, g, sine, decay, rates, hartley, waves, pre, sb, rb, sb2, rb2, ex, ey,
     f0, a0, b0, f1, a1, b1, f2, a2, b2, f3, a3, b3, f4, a4,
     local_sem, plane_send, plane_recv, halo_send, halo_recv,
     go_send, go_recv, back_send, back_recv,
@@ -213,31 +217,21 @@
 
     rows = pl.ds(1, bx)
 
-    def halo(ref, turn):
-        def strip(d, src, dst, to):
-            return remote(src, dst, halo_send.at[turn, d], halo_recv.at[turn, d], to)
-
-        return [
-            strip(0, ref.at[pl.ds(bx, 1)], ex.at[turn, pl.ds(0, 1)], (right, my)),
-            strip(1, ref.at[pl.ds(1, 1)], ex.at[turn, pl.ds(1, 1)], (left, my)),
-            strip(2, ref.at[rows, pl.ds(by - 1, 1)], ey.at[turn, :, pl.ds(0, 1)], (mx, above)),
-            strip(3, ref.at[rows, pl.ds(0, 1)], ey.at[turn, :, pl.ds(SUB - 1, 1)], (mx, below)),
-        ]
-
-    def add_edges(ref, turn):
-        ref[0] += ex[turn, 0]
-        ref[bx - 1] += ex[turn, 1]
-        sub = lax.broadcasted_iota(jnp.int32, (bx, SUB, depth), 1)
-        ref[:, 0:SUB] += jnp.where(sub == 0, ey[turn], 0.0)
-        ref[:, by - SUB : by] += jnp.where(sub == SUB - 1, ey[turn], 0.0)
-
-    early = halo(pa, 0)
+    def strip(d, src, dst, to):
+        return remote(src, dst, halo_send.at[d], halo_recv.at[d], to)
+
+    early = [
+        strip(0, pa.at[pl.ds(bx, 1)], ex.at[0, pl.ds(0, 1)], (right, my)),
+        strip(1, pa.at[pl.ds(1, 1)], ex.at[0, pl.ds(1, 1)], (left, my)),
+        strip(2, pa.at[rows, pl.ds(by - 1, 1)], ey.at[0, :, pl.ds(0, 1)], (mx, above)),
+        strip(3, pa.at[rows, pl.ds(0, 1)], ey.at[0, :, pl.ds(SUB - 1, 1)], (mx, below)),
+    ]
     early.append(
-        remote(fx.at[pl.ds(bx, 1)], ex.at[2, pl.ds(0, 1)], plane_send.at[0], plane_recv.at[0], (right, my))
+        remote(fx.at[pl.ds(bx, 1)], ex.at[1, pl.ds(0, 1)], plane_send.at[0], plane_recv.at[0], (right, my))
     )
     early.append(
         remote(
-            fy.at[:, pl.ds(by - 1, 1)], ey.at[2, :, pl.ds(0, 1)],
+            fy.at[:, pl.ds(by - 1, 1)], ey.at[1, :, pl.ds(0, 1)],
             plane_send.at[1], plane_recv.at[1], (mx, above),
         )
     )
@@ -276,14 +270,16 @@
     loop(4, prepare)
     for copy in early:
         copy.wait_recv()
-    add_edges(g, 0)
-    g[0] += ex[2, 0]
+    g[0] += ex[0, 0] + ex[1, 0]
+    g[bx - 1] += ex[0, 1]
     column = lax.broadcasted_iota(jnp.int32, (bx, SUB, depth), 1)
-    g[:, 0:SUB] += jnp.where(column == 0, ey[2], 0.0)
+    g[:, 0:SUB] += jnp.where(column == 0, ey[0] + ey[1], 0.0)
+    g[:, by - SUB : by] += jnp.where(column == SUB - 1, ey[0], 0.0)
 
     class Exchange:
-        def __init__(self, h, src, dst, send, recv):
-            self.h, self.src, self.dst, self.send, self.recv = h, src, dst, send, recv
+        def __init__(self, h, rows, src, dst, send, recv):
+            self.h, self.rows = h, pl.ds(0, rows)
+            self.src, self.dst, self.send, self.recv = src, dst, send, recv
 
         def copy(self, src, dst, to):
             return pltpu.make_async_remote_copy(
@@ -300,7 +296,7 @@
                 for j in range(first, ny):
                     y = my + j
                     y = jnp.where(y >= ny, y - ny, y)
-                    self.copy(src.at[x * ny + y], dst.at[me], (x, y)).start()
+                    self.copy(src.at[x * ny + y, self.rows], dst.at[me, self.rows], (x, y)).start()
 
             loop(nx - 1, lambda i: column(i + 1, 0))
             column(0, 1)
@@ -308,7 +304,7 @@
 
         def all(self):
             most = pl.ds(0, n - 1)
-            return self.copy(self.src.at[self.h, most], self.dst.at[self.h, most], (left, my))
+            return self.copy(self.src.at[self.h, most, self.rows], self.dst.at[self.h, most, self.rows], (left, my))
 
         def arrive(self):
             self.all().wait_recv()
@@ -317,10 +313,10 @@
             self.all().wait_send()
 
     def go(h):
-        return Exchange(h, sb, rb, go_send, go_recv)
+        return Exchange(h, deep * SUB, sb, rb, go_send, go_recv)
 
     def back(h):
-        return Exchange(h, sb2, rb2, back_send, back_recv)
+        return Exchange(h, deep * SUB + HALF, sb2, rb2, back_send, back_recv)
 
     def forward(h):
         modes = [to_modes(sine[h], g[pl.ds(c * (bx // 2), bx // 2)]) + pre[h, c] for c in range(2)]
@@ -329,7 +325,7 @@
             both = swap(*[m[:, part].reshape(n // 2, SUB, LANES) for m in modes])
             for parity in range(2):
                 for e in range(n // 2):
-                    sb[h, 2 * e + parity, p] = both[parity][e]
+                    sb[h, 2 * e + parity, pl.ds(p * SUB, SUB)] = both[parity][e]
         go(h).start()
 
     loop(2, forward)
@@ -338,7 +334,9 @@
         go(h).arrive()
         for x in range(nx // 2):
             for p in range(deep):
-                pairs = [swap(rb[h, x * ny + y, p], rb[h, (x + nx // 2) * ny + y, p]) for y in range(ny)]
+                pairs = [
+                    swap(tile(rb, h, x * ny + y, p), tile(rb, h, (x + nx // 2) * ny + y, p)) for y in range(ny)
+                ]
                 for c in range(2):
                     tiles = [pair[c] for pair in pairs]
                     groups = [transposed(tiles[k : k + tx], by) for k in range(0, ny, tx)]
@@ -396,9 +394,39 @@
                     kept.append(tiles)
                 for y in range(ny):
                     one, other = swap(kept[0][y], kept[1][y])
-                    sb2[h, x * ny + y, p] = one
-                    sb2[h, (x + nx // 2) * ny + y, p] = other
+                    sb2[h, x * ny + y, pl.ds(p * SUB, SUB)] = one
+                    sb2[h, (x + nx // 2) * ny + y, pl.ds(p * SUB, SUB)] = other
+        ghosts(b0, count)
+        for x in range(nx // 2):
+            lines(h, x)
         back(h).start()
+
+    def lines(h, x):
+        width = ny * by
+        lane = lax.broadcasted_iota(jnp.int32, (SUB, width), 1)
+        column = lax.rem(lane, by)
+        first = last = jnp.zeros((SUB, width), jnp.float32)
+        for i in range(bx):
+            row = b0[1 + x * bx + i]
+            first = jnp.where(column == i, pltpu.roll(row, i, 1), first)
+            last = jnp.where(column == i, pltpu.roll(row, (i + 1 - by) % width, 1), last)
+        lane = lane[:, 0:LANES]
+        for y in range(ny):
+            parts = [
+                pltpu.roll(piece, shift % width, 1)[:, 0:LANES]
+                for piece, shift in (
+                    (b0[x * bx], -y * by),
+                    (b0[1 + (x + 1) * bx], by - y * by),
+                    (last, 2 * by - (y - 1) % ny * by),
+                    (first, 2 * by + bx - (y + 1) % ny * by),
+                )
+            ]
+            line = parts[3]
+            for part, stop in zip(parts[2::-1], (2 * by + bx, 2 * by, by)):
+                line = jnp.where(lane < stop, part, line)
+            spot = pl.ds(deep * SUB, SUB)
+            sb2[h, x * ny + y, spot] = line
+            sb2[h, (x + nx // 2) * ny + y, spot] = flip(line)
 
     loop(2, solve)
 
@@ -406,7 +434,7 @@
         parts = [[], []]
         for p in range(deep):
             tiles = [
-                swap(mail[h, 2 * e, p], mail[h, 2 * e + 1, p]) for e in range(n // 2)
+                swap(tile(mail, h, 2 * e, p), tile(mail, h, 2 * e + 1, p)) for e in range(n // 2)
             ]
             for c in range(2):
                 parts[c].append(jnp.concatenate([t[c] for t in tiles], axis=0))
@@ -418,7 +446,7 @@
             yield c * (bx // 2), values.reshape(bx // 2, by, depth)
 
     def inner_remainder(h, d):
-        c = rb2[h, d]
+        c = rb2[h, d, 0 : deep * SUB].reshape(deep, SUB, LANES)
         lane = lax.broadcasted_iota(jnp.int32, c.shape, 2)
         lower = low((1, SUB, LANES))
         column = lax.rem(lane, by)
@@ -431,7 +459,9 @@
         after_y = jnp.where(column == by - 1, 0.0, pltpu.roll(c, LANES - 1, 2))
         before_y = jnp.where(column == 0, 0.0, pltpu.roll(c, 1, 2))
         lam = rates[h, pl.ds(pl.multiple_of(d * SUB, SUB), SUB)][None]
-        rb[h, d] = (sb[h, d] - lam * c) - (4.0 * c - ((after + before) + (after_y + before_y)))
+        f = sb[h, d].reshape(deep, SUB, LANES)
+        r = (f - lam * c) - (4.0 * c - ((after + before) + (after_y + before_y)))
+        rb[h, d] = r.reshape(deep * SUB, LANES)
 
     def remainders(h):
         def several(i):
@@ -440,25 +470,37 @@
 
         loop(n // 8, several)
 
+    def add_lines(h):
+        pairs = [swap(tile(rb2, h, 2 * e, deep), tile(rb2, h, 2 * e + 1, deep)) for e in range(n // 2)]
+        values = lax.dot_general(
+            jnp.concatenate([pair[0] for pair in pairs], axis=0), sine[h], (((0,), (0,)), ((), ())),
+            preferred_element_type=jnp.float32, precision=EXACT,
+        )
+        out_r[0] += values[0:by]
+        out_r[bx - 1] += values[by : 2 * by]
+        sub = lax.broadcasted_iota(jnp.int32, (SUB, depth), 0)
+        for i in range(bx):
+            at = 2 * by + i
+            before = jnp.broadcast_to(values[at : at + 1], (SUB, depth))
+            after = jnp.broadcast_to(values[at + bx : at + bx + 1], (SUB, depth))
+            out_r[i, 0:SUB] += jnp.where(sub == 0, before, 0.0)
+            out_r[i, by - SUB : by] += jnp.where(sub == SUB - 1, after, 0.0)
+
     half = bx // 2
-    back(0).arrive()
-    for r, values in to_cells(rb2, 0):
-        da[pl.ds(1 + r, half)] = values
-    remainders(0)
-    for r, values in to_cells(rb, 0):
-        out_r[pl.ds(r, half)] = values
-    back(1).arrive()
-    for r, values in to_cells(rb2, 1):
-        da[pl.ds(1 + r, half)] += values
-    late = halo(da, 1)
-    remainders(1)
-    for r, values in to_cells(rb, 1):
-        out_r[pl.ds(r, half)] += values
-    out_p[...] = pa[pl.ds(1, bx)] + da[pl.ds(1, bx)]
-    for copy in late:
-        copy.wait_recv()
-    add_edges(out_r, 1)
-    for copy in early + late:
+
+    def home(h, first):
+        back(h).arrive()
+        for r, values in to_cells(rb2, h):
+            old = pa[pl.ds(1 + r, half)] if first else out_p[pl.ds(r, half)]
+            out_p[pl.ds(r, half)] = old + values
+        remainders(h)
+        for r, values in to_cells(rb, h):
+            out_r[pl.ds(r, half)] = values if first else out_r[pl.ds(r, half)] + values
+        add_lines(h)
+
+    home(0, True)
+    home(1, False)
+    for copy in early:
         copy.wait_send()
     for h in range(2):
         go(h).finish()
@@ -522,14 +564,15 @@
         levels += [vmem(nx * bx // 2 // 2**level + 2, SUB, width)] * count
     scratch = (
         [vmem(bx + 1, by, depth), vmem(*block), vmem(*block)]
-        + [vmem(bx + 2, by, depth)] * 2
+        + [vmem(bx + 2, by, depth)]
         + [vmem(*block)]
         + [vmem(*c.shape) for c in constants]
         + [vmem(2, 2, n * HALF, bx // 2 * by)]
-        + [vmem(2, n, deep, SUB, LANES)] * 4
-        + [vmem(3, 2, by, depth), vmem(3, bx, SUB, depth)]
+        + [vmem(2, n, deep * SUB, LANES)] * 2
+        + [vmem(2, n, (deep + 1) * SUB, LANES)] * 2
+        + [vmem(2, 2, by, depth), vmem(2, bx, SUB, depth)]
         + levels
-        + [sem((14,)), sem((2,)), sem((2,)), sem((2, 4)), sem((2, 4))]
+        + [sem((14,)), sem((2,)), sem((2,)), sem((4,)), sem((4,))]
         + [sem((2,))] * 4
     )
     shape = jax.ShapeDtypeStruct(block, f32)

time: 46.6 us -> 43.6 us (0.936)
  the two profiles are of different devices: /device:TPU:0 before, /device:TPU:25 now
where the time goes in v4:
time: 43.6 us; the launch traced here: 43.5 us
  Pallas kernels  41.2 us (94%)
  local copies, waits for them, and re-layouts  1.59 us (4%)
  between operations  0.64 us (1%)
    pallas_call x1, Pallas kernels, on_device(): pl.pallas_call(functools.partial(kernel, nx, ny), out_shape=(shape, shape...  41.2 us
    unnamed x2, local copies, waits for them, and re-layouts  1.59 us

profile of v4, /device:TPU:25, one launch (start us, length us, event | category | flops | bytes accessed | tf_op | source)
XLA Modules:
  0.0 43.5 jit_solution(3979094010382361556)
XLA Ops:
  0.6 41.2 %shard_map.50 = (f32[16,32,256]{2,1,0:T(8,128)S(1)}, f32[16,32,256]{2,1,0:T(8,128)S(1)}) custom-call(f32[3,16,32,256]{3,2,1,0:T(8,128)} %forces.1, f32[16,32,256]{2,1,0:T(8,128)} %pressure.1, f32[1360,256]{1,0:T(8,128)} %constant.2.clone.tables), custom_call_target="tpu_custom_call" | custom-call | tf_op jit(solution)/shard_map/pallas_call | solution.py:581
  41.9 0.8 %copy.7 = f32[16,32,256]{2,1,0:T(8,128)} copy(f32[16,32,256]{2,1,0:T(8,128)S(1)} %get-tuple-element.4) | data formatting | bytes 1048576
  42.7 0.8 %copy.8 = f32[16,32,256]{2,1,0:T(8,128)} copy(f32[16,32,256]{2,1,0:T(8,128)S(1)} %get-tuple-element.5) | data formatting | bytes 1048576

commit v5 on v4

--- a/solution.py
+++ b/solution.py
@@ -15,6 +15,7 @@
 COARSE_SWEEPS = 4
 SUB = 8
 HALF = 4
+QUARTER = 32
 LANES = 128
 MESH = pl.DeviceIdType.MESH
 EXACT = lax.Precision.HIGHEST
@@ -59,6 +60,27 @@
 
 def tile(mail, h, d, p):
     return mail[h, d, pl.ds(p * SUB, SUB)]
+
+
+def packed(line):
+    mode = lax.rem(lax.broadcasted_iota(jnp.int32, line.shape, 0), HALF)
+    lane = lax.broadcasted_iota(jnp.int32, line.shape, 1)
+    out = line
+    for i in range(HALF - 1):
+        moved = pltpu.roll(pltpu.roll(line, SUB - HALF + 1 + i, 0), (HALF - 1 - i) * QUARTER, 1)
+        out = jnp.where((lane >= LANES - QUARTER) & (mode == i), moved, out)
+    return out
+
+
+def unpacked(line):
+    mode = lax.rem(lax.broadcasted_iota(jnp.int32, line.shape, 0), HALF)
+    lane = lax.broadcasted_iota(jnp.int32, line.shape, 1)
+    out = line
+    for i in range(HALF - 1):
+        moved = pltpu.roll(pltpu.roll(line, HALF - 1 - i, 0), (i + 1) * QUARTER, 1)
+        here = (lane >= i * QUARTER) & (lane < (i + 1) * QUARTER)
+        out = jnp.where(here & (mode == HALF - 1), moved, out)
+    return out
 
 
 class Level:
@@ -316,7 +338,7 @@
         return Exchange(h, deep * SUB, sb, rb, go_send, go_recv)
 
     def back(h):
-        return Exchange(h, deep * SUB + HALF, sb2, rb2, back_send, back_recv)
+        return Exchange(h, deep * SUB + HALF - 1, sb2, rb2, back_send, back_recv)
 
     def forward(h):
         modes = [to_modes(sine[h], g[pl.ds(c * (bx // 2), bx // 2)]) + pre[h, c] for c in range(2)]
@@ -424,6 +446,7 @@
             line = parts[3]
             for part, stop in zip(parts[2::-1], (2 * by + bx, 2 * by, by)):
                 line = jnp.where(lane < stop, part, line)
+            line = packed(line)
             spot = pl.ds(deep * SUB, SUB)
             sb2[h, x * ny + y, spot] = line
             sb2[h, (x + nx // 2) * ny + y, spot] = flip(line)
@@ -458,22 +481,29 @@
         before = jnp.where(lane < by, jnp.concatenate([beyond, before[:-1]], axis=0), before)
         after_y = jnp.where(column == by - 1, 0.0, pltpu.roll(c, LANES - 1, 2))
         before_y = jnp.where(column == 0, 0.0, pltpu.roll(c, 1, 2))
-        lam = rates[h, pl.ds(pl.multiple_of(d * SUB, SUB), SUB)][None]
+        at = d * SUB if isinstance(d, int) else pl.multiple_of(d * SUB, SUB)
+        lam = rates[h, pl.ds(at, SUB)][None]
         f = sb[h, d].reshape(deep, SUB, LANES)
         r = (f - lam * c) - (4.0 * c - ((after + before) + (after_y + before_y)))
         rb[h, d] = r.reshape(deep * SUB, LANES)
 
     def remainders(h):
+        group = min(n, 32)
+        if n == group:
+            for d in range(n):
+                inner_remainder(h, d)
+            return
+
         def several(i):
-            for j in range(8):
-                inner_remainder(h, 8 * i + j)
-
-        loop(n // 8, several)
+            for j in range(group):
+                inner_remainder(h, group * i + j)
+
+        loop(n // group, several)
 
     def add_lines(h):
         pairs = [swap(tile(rb2, h, 2 * e, deep), tile(rb2, h, 2 * e + 1, deep)) for e in range(n // 2)]
         values = lax.dot_general(
-            jnp.concatenate([pair[0] for pair in pairs], axis=0), sine[h], (((0,), (0,)), ((), ())),
+            jnp.concatenate([unpacked(pair[0]) for pair in pairs], axis=0), sine[h], (((0,), (0,)), ((), ())),
             preferred_element_type=jnp.float32, precision=EXACT,
         )
         out_r[0] += values[0:by]

time: 43.6 us -> 42.2 us (0.968)
  Pallas kernels: 41.2 us -> 39.8 us
    pallas_call x1, Pallas kernels: 41.2 us -> 39.8 us  [on_device(): pl.pallas_call(functools.partial(kernel, nx, ny), out_shape=(shape, shape...]
where the time goes in v5:
time: 42.2 us; the launch traced here: 42.1 us
  Pallas kernels  39.8 us (94%)
  local copies, waits for them, and re-layouts  1.59 us (4%)
  between operations  0.64 us (2%)
    pallas_call x1, Pallas kernels, on_device(): pl.pallas_call(functools.partial(kernel, nx, ny), out_shape=(shape, shape...  39.8 us
    unnamed x2, local copies, waits for them, and re-layouts  1.59 us

profile of v5, /device:TPU:25, one launch (start us, length us, event | category | flops | bytes accessed | tf_op | source)
XLA Modules:
  0.0 42.1 jit_solution(14892262122091355790)
XLA Ops:
  0.6 39.8 %shard_map.50 = (f32[16,32,256]{2,1,0:T(8,128)S(1)}, f32[16,32,256]{2,1,0:T(8,128)S(1)}) custom-call(f32[3,16,32,256]{3,2,1,0:T(8,128)} %forces.1, f32[16,32,256]{2,1,0:T(8,128)} %pressure.1, f32[1360,256]{1,0:T(8,128)} %constant.2.clone.tables), custom_call_target="tpu_custom_call" | custom-call | tf_op jit(solution)/shard_map/pallas_call | solution.py:611
  40.5 0.8 %copy.7 = f32[16,32,256]{2,1,0:T(8,128)} copy(f32[16,32,256]{2,1,0:T(8,128)S(1)} %get-tuple-element.4) | data formatting | bytes 1048576
  41.3 0.8 %copy.8 = f32[16,32,256]{2,1,0:T(8,128)} copy(f32[16,32,256]{2,1,0:T(8,128)S(1)} %get-tuple-element.5) | data formatting | bytes 1048576

commit v6 on v5

--- a/solution.py
+++ b/solution.py
@@ -179,9 +179,9 @@
 def kernel(
     nx, ny,
     forces, pressure, tables, out_p, out_r,
-    fx, fy, fz, pa, g, sine, decay, rates, hartley, waves, pre, sb, rb, sb2, rb2, ex, ey,
+    fx, fy, fz, pa, g, sine, decay, rates, hartley, waves, pre, sb, rb, sb2, rb2, edge, ex, ey,
     f0, a0, b0, f1, a1, b1, f2, a2, b2, f3, a3, b3, f4, a4,
-    local_sem, plane_send, plane_recv, halo_send, halo_recv,
+    local_sem, halo_send, halo_recv,
     go_send, go_recv, back_send, back_recv,
 ):
     mx, my = lax.axis_index("gx"), lax.axis_index("gy")
@@ -224,6 +224,7 @@
     pa[bx + 1] = jnp.zeros((by, depth), jnp.float32)
     for load in loads[:3]:
         load.wait()
+    edge[0] = pa[bx] + fx[bx]
     pl.semaphore_wait(barrier, n - 1)
 
     right, left = lax.rem(mx + 1, nx), lax.rem(mx + nx - 1, nx)
@@ -243,18 +244,15 @@
         return remote(src, dst, halo_send.at[d], halo_recv.at[d], to)
 
     early = [
-        strip(0, pa.at[pl.ds(bx, 1)], ex.at[0, pl.ds(0, 1)], (right, my)),
-        strip(1, pa.at[pl.ds(1, 1)], ex.at[0, pl.ds(1, 1)], (left, my)),
+        strip(0, edge, ex.at[pl.ds(0, 1)], (right, my)),
+        strip(1, pa.at[pl.ds(1, 1)], ex.at[pl.ds(1, 1)], (left, my)),
         strip(2, pa.at[rows, pl.ds(by - 1, 1)], ey.at[0, :, pl.ds(0, 1)], (mx, above)),
         strip(3, pa.at[rows, pl.ds(0, 1)], ey.at[0, :, pl.ds(SUB - 1, 1)], (mx, below)),
     ]
     early.append(
-        remote(fx.at[pl.ds(bx, 1)], ex.at[1, pl.ds(0, 1)], plane_send.at[0], plane_recv.at[0], (right, my))
-    )
-    early.append(
         remote(
             fy.at[:, pl.ds(by - 1, 1)], ey.at[1, :, pl.ds(0, 1)],
-            plane_send.at[1], plane_recv.at[1], (mx, above),
+            halo_send.at[4], halo_recv.at[4], (mx, above),
         )
     )
     for load in loads[3:]:
@@ -292,8 +290,8 @@
     loop(4, prepare)
     for copy in early:
         copy.wait_recv()
-    g[0] += ex[0, 0] + ex[1, 0]
-    g[bx - 1] += ex[0, 1]
+    g[0] += ex[0]
+    g[bx - 1] += ex[1]
     column = lax.broadcasted_iota(jnp.int32, (bx, SUB, depth), 1)
     g[:, 0:SUB] += jnp.where(column == 0, ey[0] + ey[1], 0.0)
     g[:, by - SUB : by] += jnp.where(column == SUB - 1, ey[0], 0.0)
@@ -600,9 +598,9 @@
         + [vmem(2, 2, n * HALF, bx // 2 * by)]
         + [vmem(2, n, deep * SUB, LANES)] * 2
         + [vmem(2, n, (deep + 1) * SUB, LANES)] * 2
-        + [vmem(2, 2, by, depth), vmem(2, bx, SUB, depth)]
+        + [vmem(1, by, depth), vmem(2, by, depth), vmem(2, bx, SUB, depth)]
         + levels
-        + [sem((14,)), sem((2,)), sem((2,)), sem((4,)), sem((4,))]
+        + [sem((14,)), sem((5,)), sem((5,))]
         + [sem((2,))] * 4
     )
     shape = jax.ShapeDtypeStruct(block, f32)

time: 42.2 us -> 41 us (0.972)
  Pallas kernels: 39.8 us -> 38.6 us
    pallas_call x1, Pallas kernels: 39.8 us -> 38.6 us  [on_device(): pl.pallas_call(functools.partial(kernel, nx, ny), out_shape=(shape, shape...]
where the time goes in v6:
time: 41 us; the launch traced here: 40.8 us
  Pallas kernels  38.6 us (94%)
  local copies, waits for them, and re-layouts  1.59 us (4%)
  between operations  0.64 us (2%)
    pallas_call x1, Pallas kernels, on_device(): pl.pallas_call(functools.partial(kernel, nx, ny), out_shape=(shape, shape...  38.6 us
    unnamed x2, local copies, waits for them, and re-layouts  1.59 us

profile of v6, /device:TPU:25, one launch (start us, length us, event | category | flops | bytes accessed | tf_op | source)
XLA Modules:
  0.0 40.8 jit_solution(6679778950759414081)
XLA Ops:
  0.6 38.6 %shard_map.50 = (f32[16,32,256]{2,1,0:T(8,128)S(1)}, f32[16,32,256]{2,1,0:T(8,128)S(1)}) custom-call(f32[3,16,32,256]{3,2,1,0:T(8,128)} %forces.1, f32[16,32,256]{2,1,0:T(8,128)} %pressure.1, f32[1360,256]{1,0:T(8,128)} %constant.2.clone.tables), custom_call_target="tpu_custom_call" | custom-call | tf_op jit(solution)/shard_map/pallas_call | solution.py:609
  39.3 0.8 %copy.7 = f32[16,32,256]{2,1,0:T(8,128)} copy(f32[16,32,256]{2,1,0:T(8,128)S(1)} %get-tuple-element.4) | data formatting | bytes 1048576
  40.0 0.8 %copy.8 = f32[16,32,256]{2,1,0:T(8,128)} copy(f32[16,32,256]{2,1,0:T(8,128)S(1)} %get-tuple-element.5) | data formatting | bytes 1048576
